TPU v7x, 32 devices: a whole 2x2x4 slice. The times are simulated.
32 devices in a mesh: lat: 2 (over y), lon: 4 (over x, core), lev: 4 (over z).
Axes of the slice: x: 2, y: 2, z: 4, core: 2. Of those that a mesh axis runs over, the one named last changes fastest.
Arguments:
- tracer: float32 [8, 512, 128, 128], P('lat', 'lon', 'lev'), may hold values from 0.5 to 2
- conductance: float32 [8, 512, 128, 128], P('lat', 'lon', 'lev'), may hold values from 0.03 to 0.15
- source: float32 [8, 512, 128, 128], P('lat', 'lon', 'lev'), may hold values from -0.2 to 0.2
Outputs:
- standardized: float32 [8, 512, 128, 128], P('lat', 'lon', 'lev')
- tracer_end: float32 [8, 512, 128, 128], P('lat', 'lon', 'lev')
All inputs are finite; a program needn't handle non-finite values.
Results may differ from a plain program's by a relative error of at most 0.00002.
Values sent between devices are 32-bit elements; how exact they have to be, the bound alone decides.
A program may use at most 128 MiB of HBM per device.

v0:
```python
import functools

import jax
import jax.numpy as jnp
from jax import lax
from jax.experimental import pallas as pl
from jax.experimental.pallas import tpu as pltpu
from jax.sharding import PartitionSpec as P

STEPS = 3
GUESS = 1.0
TILE = 8
ROWS = 8


def kernel(
    sizes, tracer, conductance, source, end, mean_out, scale_out,
    even, odd, cond, sour, z_lower, z_upper, z_first, z_last, sums, peer_sums,
    load_sem, y_send, y_recv, x_send, x_recv, z_send, z_recv, sum_send, sum_recv,
):
    n_lat, n_lon, n_lev = sizes
    J, I, K, M = tracer.shape
    chunks = K // TILE
    blocks = I // ROWS
    count = I * n_lon
    lat, lon, lev = lax.axis_index("lat"), lax.axis_index("lon"), lax.axis_index("lev")
    below = {"lat": lat > 0, "lon": lon > 0, "lev": lev > 0}
    above = {"lat": lat < n_lat - 1, "lon": lon < n_lon - 1, "lev": lev < n_lev - 1}
    index = {"lat": lat, "lon": lon, "lev": lev}
    field = [even, odd]

    def levels(chunk):
        return pl.ds(chunk * TILE, TILE)

    def target(axis, way):
        return {axis: index[axis] + (1 if way == 0 else -1)}

    def y_copy(step, chunk, way):
        plane = J - 1 if way == 0 else 0
        if step == 0:
            src = tracer.at[plane, :, levels(chunk), :]
        else:
            src = field[step % 2].at[plane + 1, pl.ds(1, I), levels(chunk), :]
        dst = field[step % 2].at[0 if way == 0 else J + 1, pl.ds(1, I), levels(chunk), :]
        return pltpu.make_async_remote_copy(
            src_ref=src, dst_ref=dst, send_sem=y_send.at[step, chunk, way],
            recv_sem=y_recv.at[step, chunk, way], device_id=target("lat", way),
            device_id_type=pl.DeviceIdType.MESH)

    def x_copy(step, way):
        buf = field[step % 2]
        return pltpu.make_async_remote_copy(
            src_ref=buf.at[pl.ds(1, J), I if way == 0 else 1],
            dst_ref=buf.at[pl.ds(1, J), 0 if way == 0 else I + 1],
            send_sem=x_send.at[step, way], recv_sem=x_recv.at[step, way],
            device_id=target("lon", way), device_id_type=pl.DeviceIdType.MESH)

    def z_copy(step, way):
        src = z_last if way == 0 else z_first
        dst = z_lower if way == 0 else z_upper
        return pltpu.make_async_remote_copy(
            src_ref=src.at[step % 2], dst_ref=dst.at[step % 2],
            send_sem=z_send.at[step, way], recv_sem=z_recv.at[step, way],
            device_id=target("lev", way), device_id_type=pl.DeviceIdType.MESH)

    early = jnp.where(lat == 0, 0, J - 1)
    late = J - 1 - early
    parts = [pl.ds(jnp.where(lat == 0, 0, 1), J - 1), pl.ds(late, 1)]

    def sum_copy(chunk, shift, part):
        return pltpu.make_async_remote_copy(
            src_ref=sums.at[chunk, parts[part]],
            dst_ref=peer_sums.at[shift - 1, chunk, parts[part]],
            send_sem=sum_send.at[chunk, shift - 1, part],
            recv_sem=sum_recv.at[chunk, shift - 1, part],
            device_id={"lon": lax.rem(lon + shift, n_lon)}, device_id_type=pl.DeviceIdType.MESH)

    def sends(axis, way, act):
        pl.when((above if way == 0 else below)[axis])(act)

    def arrives(axis, way, act):
        pl.when((below if way == 0 else above)[axis])(act)

    barrier = pltpu.get_barrier_semaphore()
    met = n_lon - 1
    for axis in ("lat", "lev"):
        for way in (0, 1):
            def greet(axis=axis, way=way):
                pl.semaphore_signal(barrier, inc=1, device_id=target(axis, way),
                                    device_id_type=pl.DeviceIdType.MESH)
            sends(axis, way, greet)
        met = met + below[axis].astype(jnp.int32) + above[axis].astype(jnp.int32)
    for shift in range(1, n_lon):
        pl.semaphore_signal(barrier, inc=1, device_id={"lon": lax.rem(lon + shift, n_lon)},
                            device_id_type=pl.DeviceIdType.MESH)

    loads = [
        pltpu.make_async_copy(tracer, even.at[pl.ds(1, J), pl.ds(1, I)], load_sem.at[0]),
        pltpu.make_async_copy(conductance, cond, load_sem.at[1]),
        pltpu.make_async_copy(source, sour, load_sem.at[2]),
    ]
    loads[0].start()
    pl.semaphore_wait(barrier, met)

    for chunk in range(chunks):
        for way in (0, 1):
            sends("lat", way, lambda: y_copy(0, chunk, way).start())
    loads[1].start()
    loads[2].start()

    for way in (0, 1):
        def no_y():
            @pl.loop(0, blocks)
            def _(b):
                for buf in field:
                    buf[0 if way == 0 else J + 1, pl.ds(1 + b * ROWS, ROWS)] = jnp.zeros(
                        (ROWS, K, M), jnp.float32)
        pl.when(jnp.logical_not((below if way == 0 else above)["lat"]))(no_y)

        def no_x():
            for buf in field:
                for j in range(J):
                    buf[1 + j, 0 if way == 0 else I + 1] = jnp.zeros((K, M), jnp.float32)
        pl.when(jnp.logical_not((below if way == 0 else above)["lon"]))(no_x)

        def no_z():
            @pl.loop(0, blocks)
            def _(b):
                for p in range(2):
                    for j in range(J):
                        (z_lower if way == 0 else z_upper)[p, j, pl.ds(b * ROWS, ROWS)] = (
                            jnp.zeros((ROWS, 1, M), jnp.float32))
        pl.when(jnp.logical_not((below if way == 0 else above)["lev"]))(no_z)

    def pack_and_send(step):
        buf = field[step % 2]
        for way in (0, 1):
            sends("lon", way, lambda: x_copy(step, way).start())

        @pl.loop(0, J * blocks)
        def _(q):
            j, r = q // blocks, (q % blocks) * ROWS
            z_first[step % 2, j, pl.ds(r, ROWS)] = buf[1 + j, pl.ds(1 + r, ROWS), pl.ds(0, 1), :]
            z_last[step % 2, j, pl.ds(r, ROWS)] = buf[1 + j, pl.ds(1 + r, ROWS), pl.ds(K - 1, 1), :]

        for way in (0, 1):
            sends("lev", way, lambda: z_copy(step, way).start())

    def next_rows(step, chunk, j, r):
        buf = field[step % 2]
        here = levels(chunk)
        mid = buf[1 + j, pl.ds(1 + r, ROWS), here, :]
        k = lax.broadcasted_iota(jnp.int32, mid.shape, 1)
        if chunk == 0:
            edge = jnp.broadcast_to(z_lower[step % 2, j, pl.ds(r, ROWS)], mid.shape)
        else:
            edge = pltpu.roll(buf[1 + j, pl.ds(1 + r, ROWS), levels(chunk - 1), :], 1, 1)
        k_lower = jnp.where(k == 0, edge, pltpu.roll(mid, 1, 1))
        if chunk == chunks - 1:
            edge = jnp.broadcast_to(z_upper[step % 2, j, pl.ds(r, ROWS)], mid.shape)
        else:
            edge = pltpu.roll(buf[1 + j, pl.ds(1 + r, ROWS), levels(chunk + 1), :], TILE - 1, 1)
        k_upper = jnp.where(k == TILE - 1, edge, pltpu.roll(mid, TILE - 1, 1))
        spread = (
            buf[j, pl.ds(1 + r, ROWS), here, :] + buf[2 + j, pl.ds(1 + r, ROWS), here, :]
            + buf[1 + j, pl.ds(r, ROWS), here, :] + buf[1 + j, pl.ds(2 + r, ROWS), here, :]
            + k_lower + k_upper - 6.0 * mid)
        return mid + cond[j, pl.ds(r, ROWS), here, :] * spread + sour[j, pl.ds(r, ROWS), here, :]

    def planes(step, chunk, first, number):
        if step < STEPS - 1:
            to = field[(step + 1) % 2]

            @pl.loop(0, number * blocks)
            def _(q):
                j, r = first + q // blocks, (q % blocks) * ROWS
                to[1 + j, pl.ds(1 + r, ROWS), levels(chunk), :] = next_rows(step, chunk, j, r)
        else:
            @pl.loop(0, number)
            def _(p):
                j = first + p

                def body(b, totals):
                    new = next_rows(step, chunk, j, b * ROWS)
                    end[j, pl.ds(b * ROWS, ROWS), levels(chunk), :] = new
                    moved = new - GUESS
                    return (totals[0] + jnp.sum(moved, axis=0),
                            totals[1] + jnp.sum(moved * moved, axis=0))

                zero = jnp.zeros((TILE, M), jnp.float32)
                total, square = lax.fori_loop(0, blocks, body, (zero, zero))
                sums[chunk, j, 0] = total
                sums[chunk, j, 1] = square

    def y_arrives(step, chunk, way):
        arrives("lat", way, lambda: y_copy(step, chunk, way).wait_recv())

    loads[0].wait()
    pack_and_send(0)
    loads[1].wait()
    loads[2].wait()
    for step in range(STEPS):
        if step >= 1:
            for way in (0, 1):
                sends("lon", way, lambda: x_copy(step - 1, way).wait_send())
                sends("lev", way, lambda: z_copy(step - 1, way).wait_send())
                for chunk in range(chunks):
                    sends("lat", way, lambda: y_copy(step - 1, chunk, way).wait_send())
        for way in (0, 1):
            arrives("lon", way, lambda: x_copy(step, way).wait_recv())
            arrives("lev", way, lambda: z_copy(step, way).wait_recv())
        if step == STEPS - 1:
            for chunk in range(chunks):
                planes(step, chunk, 1, J - 2)
        for chunk in range(chunks):
            if step < STEPS - 1:
                planes(step, chunk, 1, J - 2)
            pl.when(jnp.logical_and(lat > 0, lat < n_lat - 1))(
                lambda: y_copy(step, chunk, 1).wait_recv())
            planes(step, chunk, early, 1)
            if step == STEPS - 1:
                for shift in range(1, n_lon):
                    sum_copy(chunk, shift, 0).start()
            pl.when(lat > 0)(lambda: y_copy(step, chunk, 0).wait_recv())
            pl.when(jnp.logical_and(lat == 0, lat < n_lat - 1))(
                lambda: y_copy(step, chunk, 1).wait_recv())
            planes(step, chunk, late, 1)
            if step < STEPS - 1:
                for way in (0, 1):
                    sends("lat", way, lambda: y_copy(step + 1, chunk, way).start())
            else:
                for shift in range(1, n_lon):
                    sum_copy(chunk, shift, 1).start()
        if step < STEPS - 1:
            pack_and_send(step + 1)

    for chunk in range(chunks):
        for shift in range(1, n_lon):
            for part in (0, 1):
                sum_copy(chunk, shift, part).wait_recv()
        total = sums[chunk]
        for shift in range(1, n_lon):
            total = total + peer_sums[shift - 1, chunk]
        offset = total[:, 0] / count
        variance = total[:, 1] / count - offset * offset
        mean_out[:, levels(chunk), :] = GUESS + offset
        scale_out[:, levels(chunk), :] = lax.rsqrt(variance + 0.0001)

    for chunk in range(chunks):
        for shift in range(1, n_lon):
            for part in (0, 1):
                sum_copy(chunk, shift, part).wait_send()
        for way in (0, 1):
            sends("lat", way, lambda: y_copy(STEPS - 1, chunk, way).wait_send())
    for way in (0, 1):
        sends("lon", way, lambda: x_copy(STEPS - 1, way).wait_send())
        sends("lev", way, lambda: z_copy(STEPS - 1, way).wait_send())


def write_out(end, mean, scale, standardized, end_out, held, sem):
    J, I, K, M = end.shape
    keep = pltpu.make_async_copy(end, end_out, sem.at[J])
    keep.start()
    copies = []
    for j in range(J):
        offset, factor = mean[j], scale[j]

        @pl.loop(0, I // ROWS)
        def _(b):
            rows = pl.ds(b * ROWS, ROWS)
            held[j, rows] = (end[j, rows] - offset) * factor

        copies.append(pltpu.make_async_copy(held.at[j], standardized.at[j], sem.at[j]))
        copies[-1].start()
    for copy in copies + [keep]:
        copy.wait()


def shards(sizes, tracer, conductance, source):
    n_lat, n_lon, n_lev = sizes
    J, I, K, M = tracer.shape
    chunks = K // TILE
    f32 = jnp.float32
    dma = pltpu.SemaphoreType.DMA
    peers = max(n_lon - 1, 1)
    end, mean, scale = pl.pallas_call(
        functools.partial(kernel, sizes),
        out_shape=[
            pltpu.VMEM((J, I, K, M), f32),
            pltpu.VMEM((J, K, M), f32),
            pltpu.VMEM((J, K, M), f32),
        ],
        in_specs=[pl.BlockSpec(memory_space=pltpu.HBM)] * 3,
        out_specs=[pl.BlockSpec(memory_space=pltpu.VMEM)] * 3,
        scratch_shapes=[
            pltpu.VMEM((J + 2, I + 2, K, M), f32),
            pltpu.VMEM((J + 2, I + 2, K, M), f32),
            pltpu.VMEM((J, I, K, M), f32),
            pltpu.VMEM((J, I, K, M), f32),
            pltpu.VMEM((2, J, I, 1, M), f32),
            pltpu.VMEM((2, J, I, 1, M), f32),
            pltpu.VMEM((2, J, I, 1, M), f32),
            pltpu.VMEM((2, J, I, 1, M), f32),
            pltpu.VMEM((chunks, J, 2, TILE, M), f32),
            pltpu.VMEM((peers, chunks, J, 2, TILE, M), f32),
            dma((3,)),
            dma((STEPS, chunks, 2)),
            dma((STEPS, chunks, 2)),
            dma((STEPS, 2)),
            dma((STEPS, 2)),
            dma((STEPS, 2)),
            dma((STEPS, 2)),
            dma((chunks, peers, 2)),
            dma((chunks, peers, 2)),
        ],
        compiler_params=pltpu.CompilerParams(
            collective_id=0, has_side_effects=True, vmem_limit_bytes=47 * 1024 * 1024),
    )(tracer, conductance, source)
    return pl.pallas_call(
        write_out,
        out_shape=[jax.ShapeDtypeStruct((J, I, K, M), f32)] * 2,
        in_specs=[pl.BlockSpec(memory_space=pltpu.VMEM)] * 3,
        out_specs=[pl.BlockSpec(memory_space=pltpu.HBM)] * 2,
        scratch_shapes=[pltpu.VMEM((J, I, K, M), f32), dma((J + 1,))],
        compiler_params=pltpu.CompilerParams(vmem_limit_bytes=32 * 1024 * 1024),
    )(end, mean, scale)


def solution(mesh):
    placed = P("lat", "lon", "lev", None)
    sizes = tuple(mesh.shape[axis] for axis in ("lat", "lon", "lev"))
    return jax.shard_map(
        functools.partial(shards, sizes),
        mesh=mesh,
        in_specs=(placed, placed, placed),
        out_specs=(placed, placed),
        check_vma=False,
    )
```

profile of v0, /device:TPU:0, one launch (start us, length us, event | category | flops | bytes accessed | tf_op | source)
XLA Modules:
  0.0 151.6 jit_solution(3916055887855932038)
XLA Ops:
  0.6 144.9 %shard_map.50 = (f32[4,128,32,128]{3,2,1,0:T(8,128)S(1)}, f32[4,32,128]{2,1,0:T(8,128)S(1)}, f32[4,32,128]{2,1,0:T(8,128)S(1)}) custom-call(f32[4,128,32,128]{3,2,1,0:T(8,128)} %tracer.1, f32[4,128,32,128]{3,2,1,0:T(8,128)} %conductance.1, f32[4,128,32,128]{3,2,1,0:T(8,128)} %source.1), custom_call_target="tpu_custom_call" | custom-call | tf_op jit(solution)/shard_map/pallas_call | solution.py:286
  145.6 6.0 %shard_map.51 = (f32[4,128,32,128]{3,2,1,0:T(8,128)}, f32[4,128,32,128]{3,2,1,0:T(8,128)}) custom-call(f32[4,128,32,128]{3,2,1,0:T(8,128)S(1)} %get-tuple-element.5.end, f32[4,32,128]{2,1,0:T(8,128)S(1)} %get-tuple-element.6.mean, f32[4,32,128]{2,1,0:T(8,128)S(1)} %get-tuple-element.7.scale), custom_call_target="tpu_custom_call" | custom-call | tf_op jit(solution)/shard_map/pallas_call | solution.py:319
where the time goes:
time: 152 us
  Pallas kernels  151 us (99%)
    pallas_call x1, Pallas kernels, shards(): pl.pallas_call(functools.partial(kernel, sizes), out_shape=[pltpu.VMEM((J...  145 us
    pallas_call x1, Pallas kernels, shards(): pl.pallas_call(write_out, out_shape=[jax.ShapeDtypeStruct((J, I, K, M), f...  6.02 us

commit v1 on v0

v1 whole, which is shorter than its diff:
```python
import functools

import jax
import jax.numpy as jnp
from jax import lax
from jax.experimental import pallas as pl
from jax.experimental.pallas import tpu as pltpu
from jax.sharding import PartitionSpec as P

STEPS = 3
GUESS = 1.0
TILE = 8
ROWS = 8
MESH = pl.DeviceIdType.MESH


def lat_sides(n_lat, lat, J):
    if n_lat == 2:
        return [(jnp.where(lat == 0, J - 1, 0), jnp.where(lat == 0, J - 2, 1), 1 - lat, None, 0)]
    return [(0, 1, lat - 1, lat > 0, 1), (J - 1, J - 2, lat + 1, lat < n_lat - 1, 0)]


def early_planes(n_lat, lat, J):
    if n_lat == 2:
        return jnp.where(lat == 0, 0, 1), J - 1
    return 1, J - 2


def when(condition, act):
    if condition is None:
        act()
    else:
        pl.when(condition)(act)


def kernel(
    sizes, tracer, conductance, source, end, mean_out, scale_out,
    even, odd, cond, sour, base, y_halo, z_lower, z_upper, z_first, z_last,
    sums_early, peer_early, sums_late, peer_late,
    load_sem, y_send, y_recv, x_send, x_recv, z_send, z_recv, early_send, early_recv, late_send, late_recv,
):
    n_lat, n_lon, n_lev = sizes
    J, I, K, M = tracer.shape
    chunks = K // TILE
    blocks = I // ROWS
    count = I * n_lon
    lat, lon, lev = lax.axis_index("lat"), lax.axis_index("lon"), lax.axis_index("lev")
    below = {"lon": lon > 0, "lev": lev > 0}
    above = {"lon": lon < n_lon - 1, "lev": lev < n_lev - 1}
    index = {"lon": lon, "lev": lev}
    field = [even, odd]
    sides = lat_sides(n_lat, lat, J)
    first, number = early_planes(n_lat, lat, J)
    rows_in = pl.ds(1, I)

    def levels(chunk):
        return pl.ds(chunk * TILE, TILE)

    def target(axis, way):
        return {axis: index[axis] + (1 if way == 0 else -1)}

    def y_copy(step, chunk, s):
        plane, _, peer, _, slot = sides[s]
        return pltpu.make_async_remote_copy(
            src_ref=field[step % 2].at[plane, rows_in, levels(chunk), :],
            dst_ref=y_halo.at[step % 2, slot, :, levels(chunk), :],
            send_sem=y_send.at[step, chunk, s], recv_sem=y_recv.at[step, chunk, slot],
            device_id={"lat": peer}, device_id_type=MESH)

    def y_arrival(step, chunk, s):
        plane, _, peer, _, _ = sides[s]
        return pltpu.make_async_remote_copy(
            src_ref=field[step % 2].at[plane, rows_in, levels(chunk), :],
            dst_ref=y_halo.at[step % 2, s, :, levels(chunk), :],
            send_sem=y_send.at[step, chunk, s], recv_sem=y_recv.at[step, chunk, s],
            device_id={"lat": peer}, device_id_type=MESH)

    def x_copy(step, way):
        buf = field[step % 2]
        return pltpu.make_async_remote_copy(
            src_ref=buf.at[:, I if way == 0 else 1],
            dst_ref=buf.at[:, 0 if way == 0 else I + 1],
            send_sem=x_send.at[step, way], recv_sem=x_recv.at[step, way],
            device_id=target("lon", way), device_id_type=MESH)

    def z_copy(step, way):
        src = z_last if way == 0 else z_first
        dst = z_lower if way == 0 else z_upper
        return pltpu.make_async_remote_copy(
            src_ref=src.at[step % 2], dst_ref=dst.at[step % 2],
            send_sem=z_send.at[step, way], recv_sem=z_recv.at[step, way],
            device_id=target("lev", way), device_id_type=MESH)

    def early_copy(shift):
        return pltpu.make_async_remote_copy(
            src_ref=sums_early, dst_ref=peer_early.at[shift - 1],
            send_sem=early_send.at[shift - 1], recv_sem=early_recv.at[shift - 1],
            device_id={"lon": lax.rem(lon + shift, n_lon)}, device_id_type=MESH)

    def late_copy(chunk, shift):
        return pltpu.make_async_remote_copy(
            src_ref=sums_late.at[chunk], dst_ref=peer_late.at[shift - 1, chunk],
            send_sem=late_send.at[chunk, shift - 1], recv_sem=late_recv.at[chunk, shift - 1],
            device_id={"lon": lax.rem(lon + shift, n_lon)}, device_id_type=MESH)

    def sends(axis, way, act):
        pl.when((above if way == 0 else below)[axis])(act)

    def arrives(axis, way, act):
        pl.when((below if way == 0 else above)[axis])(act)

    barrier = pltpu.get_barrier_semaphore()
    met = n_lon - 1
    for _, _, peer, exists, _ in sides:
        when(exists, lambda: pl.semaphore_signal(
            barrier, inc=1, device_id={"lat": peer}, device_id_type=MESH))
        met = met + (1 if exists is None else exists.astype(jnp.int32))
    for way in (0, 1):
        sends("lev", way, lambda: pl.semaphore_signal(
            barrier, inc=1, device_id=target("lev", way), device_id_type=MESH))
        met = met + (above if way == 0 else below)["lev"].astype(jnp.int32)
    for shift in range(1, n_lon):
        pl.semaphore_signal(barrier, inc=1, device_id={"lon": lax.rem(lon + shift, n_lon)},
                            device_id_type=MESH)

    loads = [
        pltpu.make_async_copy(tracer.at[plane], even.at[plane, rows_in], load_sem.at[3 + s])
        for s, (plane, _, _, _, _) in enumerate(sides)
    ]
    loads.append(pltpu.make_async_copy(
        tracer.at[pl.ds(first, number)], even.at[pl.ds(first, number), rows_in], load_sem.at[0]))
    loads.append(pltpu.make_async_copy(conductance, cond, load_sem.at[1]))
    loads.append(pltpu.make_async_copy(source, sour, load_sem.at[2]))
    for load in loads[:-2]:
        load.start()
    for load in loads[:-3]:
        load.wait()
    pl.semaphore_wait(barrier, met)

    for chunk in range(chunks):
        for s, side in enumerate(sides):
            when(side[3], lambda: y_copy(0, chunk, s).start())
    loads[-2].start()
    loads[-1].start()

    for s, side in enumerate(sides):
        if side[3] is not None:
            def no_y():
                @pl.loop(0, blocks)
                def _(b):
                    for p in range(2):
                        y_halo[p, s, pl.ds(b * ROWS, ROWS)] = jnp.zeros((ROWS, K, M), jnp.float32)
            pl.when(jnp.logical_not(side[3]))(no_y)
    for way in (0, 1):
        def no_x():
            for buf in field:
                for j in range(J):
                    buf[j, 0 if way == 0 else I + 1] = jnp.zeros((K, M), jnp.float32)
        pl.when(jnp.logical_not((below if way == 0 else above)["lon"]))(no_x)

        def no_z():
            @pl.loop(0, blocks)
            def _(b):
                for p in range(2):
                    for j in range(J):
                        (z_lower if way == 0 else z_upper)[p, j, pl.ds(b * ROWS, ROWS)] = (
                            jnp.zeros((ROWS, 1, M), jnp.float32))
        pl.when(jnp.logical_not((below if way == 0 else above)["lev"]))(no_z)

    def pack_and_send(step):
        buf = field[step % 2]
        for way in (0, 1):
            sends("lon", way, lambda: x_copy(step, way).start())

        @pl.loop(0, J * blocks)
        def _(q):
            j, r = q // blocks, (q % blocks) * ROWS
            z_first[step % 2, j, pl.ds(r, ROWS)] = buf[j, pl.ds(1 + r, ROWS), pl.ds(0, 1), :]
            z_last[step % 2, j, pl.ds(r, ROWS)] = buf[j, pl.ds(1 + r, ROWS), pl.ds(K - 1, 1), :]

        for way in (0, 1):
            sends("lev", way, lambda: z_copy(step, way).start())

    def next_rows(step, chunk, j, r, inward):
        buf = field[step % 2]
        here = levels(chunk)
        rows = pl.ds(1 + r, ROWS)
        mid = buf[j, rows, here, :]
        k = lax.broadcasted_iota(jnp.int32, mid.shape, 1)
        if chunk == 0:
            edge = jnp.broadcast_to(z_lower[step % 2, j, pl.ds(r, ROWS)], mid.shape)
        else:
            edge = pltpu.roll(buf[j, rows, levels(chunk - 1), :], 1, 1)
        k_lower = jnp.where(k == 0, edge, pltpu.roll(mid, 1, 1))
        if chunk == chunks - 1:
            edge = jnp.broadcast_to(z_upper[step % 2, j, pl.ds(r, ROWS)], mid.shape)
        else:
            edge = pltpu.roll(buf[j, rows, levels(chunk + 1), :], TILE - 1, 1)
        k_upper = jnp.where(k == TILE - 1, edge, pltpu.roll(mid, TILE - 1, 1))
        if inward is None:
            across = buf[j - 1, rows, here, :] + buf[j + 1, rows, here, :]
        else:
            across = buf[inward, rows, here, :]
        spread = (
            across + buf[j, pl.ds(r, ROWS), here, :] + buf[j, pl.ds(2 + r, ROWS), here, :]
            + k_lower + k_upper - 6.0 * mid)
        return mid + cond[j, pl.ds(r, ROWS), here, :] * spread + sour[j, pl.ds(r, ROWS), here, :]

    zero = jnp.zeros((TILE, M), jnp.float32)

    def tally(new, totals):
        moved = new - GUESS
        return totals[0] + jnp.sum(moved, axis=0), totals[1] + jnp.sum(moved * moved, axis=0)

    def early_plane(step, chunk, j, inward):
        def body(b, totals):
            r = b * ROWS
            new = next_rows(step, chunk, j, r, inward)
            if step < STEPS - 1:
                field[(step + 1) % 2][j, pl.ds(1 + r, ROWS), levels(chunk), :] = new
                return totals
            end[j, pl.ds(r, ROWS), levels(chunk), :] = new
            return tally(new, totals)

        if step < STEPS - 1:
            lax.fori_loop(0, blocks, lambda b, _: body(b, 0), 0)
        else:
            totals = lax.fori_loop(0, blocks, body, (zero, zero))
            for q in range(2):
                sums_early[j - first, q, levels(chunk), :] = totals[q]

    def early_part(step, chunk):
        @pl.loop(1, J - 1)
        def _(j):
            early_plane(step, chunk, j, None)

        if n_lat == 2:
            early_plane(step, chunk, jnp.where(lat == 0, 0, J - 1), jnp.where(lat == 0, 1, J - 2))
        for s, (plane, inward, _, _, _) in enumerate(sides):
            @pl.loop(0, blocks)
            def _(b):
                r = b * ROWS
                base[s, pl.ds(r, ROWS), levels(chunk), :] = next_rows(step, chunk, plane, r, inward)

    def late_part(step, chunk, s):
        plane = sides[s][0]
        here = levels(chunk)

        def body(b, totals):
            r = pl.ds(b * ROWS, ROWS)
            new = base[s, r, here, :] + cond[plane, r, here, :] * y_halo[step % 2, s, r, here, :]
            if step < STEPS - 1:
                field[(step + 1) % 2][plane, pl.ds(1 + b * ROWS, ROWS), here, :] = new
                return totals
            end[plane, r, here, :] = new
            return tally(new, totals)

        if step < STEPS - 1:
            lax.fori_loop(0, blocks, lambda b, _: body(b, 0), 0)
        else:
            totals = lax.fori_loop(0, blocks, body, (zero, zero))
            for q in range(2):
                sums_late[chunk, s, q] = totals[q]

    loads[-3].wait()
    pack_and_send(0)
    loads[-2].wait()
    loads[-1].wait()
    for step in range(STEPS):
        if step >= 1:
            for way in (0, 1):
                sends("lon", way, lambda: x_copy(step - 1, way).wait_send())
                sends("lev", way, lambda: z_copy(step - 1, way).wait_send())
            for s, side in enumerate(sides):
                for chunk in range(chunks):
                    when(side[3], lambda: y_copy(step - 1, chunk, s).wait_send())
        for way in (0, 1):
            arrives("lon", way, lambda: x_copy(step, way).wait_recv())
            arrives("lev", way, lambda: z_copy(step, way).wait_recv())
        if step == STEPS - 1:
            for way in (0, 1):
                sends("lon", way, lambda: x_copy(step, way).wait_send())
                sends("lev", way, lambda: z_copy(step, way).wait_send())
            for chunk in range(chunks):
                early_part(step, chunk)
            for shift in range(1, n_lon):
                early_copy(shift).start()
        for chunk in range(chunks):
            if step < STEPS - 1:
                early_part(step, chunk)
            for s, side in enumerate(sides):
                when(side[3], lambda: y_arrival(step, chunk, s).wait_recv())
                late_part(step, chunk, s)
                if step < STEPS - 1:
                    when(side[3], lambda: y_copy(step + 1, chunk, s).start())
            if step == STEPS - 1:
                for shift in range(1, n_lon):
                    late_copy(chunk, shift).start()
        if step < STEPS - 1:
            pack_and_send(step + 1)

    def close(total):
        offset = total[0] / count
        variance = total[1] / count - offset * offset
        return GUESS + offset, lax.rsqrt(variance + 0.0001)

    for shift in range(1, n_lon):
        early_copy(shift).wait_recv()

    @pl.loop(0, number)
    def _(p):
        total = [sums_early[p, q] for q in range(2)]
        for shift in range(1, n_lon):
            total = [total[q] + peer_early[shift - 1, p, q] for q in range(2)]
        mean_out[first + p], scale_out[first + p] = close(total)

    for shift in range(1, n_lon):
        early_copy(shift).wait_send()
    for chunk in range(chunks):
        for s, side in enumerate(sides):
            when(side[3], lambda: y_copy(STEPS - 1, chunk, s).wait_send())
    for chunk in range(chunks):
        for shift in range(1, n_lon):
            if chunk < chunks - 1:
                late_copy(chunk, shift).wait_send()
            late_copy(chunk, shift).wait_recv()
        for s, side in enumerate(sides):
            total = [sums_late[chunk, s, q] for q in range(2)]
            for shift in range(1, n_lon):
                total = [total[q] + peer_late[shift - 1, chunk, s, q] for q in range(2)]
            mean_out[side[0], levels(chunk), :], scale_out[side[0], levels(chunk), :] = close(total)
    for shift in range(1, n_lon):
        late_copy(chunks - 1, shift).wait_send()


def write_out(end, mean, scale, standardized, end_out, held, sem):
    J, I, K, M = end.shape
    copies = [pltpu.make_async_copy(end.at[j], end_out.at[j], sem.at[J + j]) for j in range(J)]
    for copy in copies:
        copy.start()
    for j in range(J):
        offset, factor = mean[j], scale[j]

        @pl.loop(0, I // ROWS)
        def _(b):
            rows = pl.ds(b * ROWS, ROWS)
            held[j, rows] = (end[j, rows] - offset) * factor

        copies.append(pltpu.make_async_copy(held.at[j], standardized.at[j], sem.at[j]))
        copies[-1].start()
    for copy in copies:
        copy.wait()


def shards(sizes, tracer, conductance, source):
    n_lat, n_lon, n_lev = sizes
    J, I, K, M = tracer.shape
    chunks = K // TILE
    f32 = jnp.float32
    dma = pltpu.SemaphoreType.DMA
    peers = max(n_lon - 1, 1)
    late = len(lat_sides(n_lat, 0, J))
    early = early_planes(n_lat, 0, J)[1]
    end, mean, scale = pl.pallas_call(
        functools.partial(kernel, sizes),
        out_shape=[
            pltpu.VMEM((J, I, K, M), f32),
            pltpu.VMEM((J, K, M), f32),
            pltpu.VMEM((J, K, M), f32),
        ],
        in_specs=[pl.BlockSpec(memory_space=pltpu.HBM)] * 3,
        out_specs=[pl.BlockSpec(memory_space=pltpu.VMEM)] * 3,
        scratch_shapes=[
            pltpu.VMEM((J, I + 2, K, M), f32),
            pltpu.VMEM((J, I + 2, K, M), f32),
            pltpu.VMEM((J, I, K, M), f32),
            pltpu.VMEM((J, I, K, M), f32),
            pltpu.VMEM((late, I, K, M), f32),
            pltpu.VMEM((2, late, I, K, M), f32),
            pltpu.VMEM((2, J, I, 1, M), f32),
            pltpu.VMEM((2, J, I, 1, M), f32),
            pltpu.VMEM((2, J, I, 1, M), f32),
            pltpu.VMEM((2, J, I, 1, M), f32),
            pltpu.VMEM((early, 2, K, M), f32),
            pltpu.VMEM((peers, early, 2, K, M), f32),
            pltpu.VMEM((chunks, late, 2, TILE, M), f32),
            pltpu.VMEM((peers, chunks, late, 2, TILE, M), f32),
            dma((3 + late,)),
            dma((STEPS, chunks, late)),
            dma((STEPS, chunks, late)),
            dma((STEPS, 2)),
            dma((STEPS, 2)),
            dma((STEPS, 2)),
            dma((STEPS, 2)),
            dma((peers,)),
            dma((peers,)),
            dma((chunks, peers)),
            dma((chunks, peers)),
        ],
        compiler_params=pltpu.CompilerParams(
            collective_id=0, has_side_effects=True, vmem_limit_bytes=50 * 1024 * 1024),
    )(tracer, conductance, source)
    return pl.pallas_call(
        write_out,
        out_shape=[jax.ShapeDtypeStruct((J, I, K, M), f32)] * 2,
        in_specs=[pl.BlockSpec(memory_space=pltpu.VMEM)] * 3,
        out_specs=[pl.BlockSpec(memory_space=pltpu.HBM)] * 2,
        scratch_shapes=[pltpu.VMEM((J, I, K, M), f32), dma((2 * J,))],
        compiler_params=pltpu.CompilerParams(vmem_limit_bytes=32 * 1024 * 1024),
    )(end, mean, scale)


def solution(mesh):
    placed = P("lat", "lon", "lev", None)
    sizes = tuple(mesh.shape[axis] for axis in ("lat", "lon", "lev"))
    return jax.shard_map(
        functools.partial(shards, sizes),
        mesh=mesh,
        in_specs=(placed, placed, placed),
        out_specs=(placed, placed),
        check_vma=False,
    )
```

time: 152 us -> 151 us (level)
  no operation moved by 1% of the time
where the time goes in v1:
time: 151 us
  Pallas kernels  150 us (99%)
    pallas_call x1, Pallas kernels, shards(): pl.pallas_call(functools.partial(kernel, sizes), out_shape=[pltpu.VMEM((J...  144 us
    pallas_call x1, Pallas kernels, shards(): pl.pallas_call(write_out, out_shape=[jax.ShapeDtypeStruct((J, I, K, M), f...  5.92 us

profile of v1, /device:TPU:0, one launch (start us, length us, event | category | flops | bytes accessed | tf_op | source)
XLA Modules:
  0.0 151.0 jit_solution(4031286307788597293)
XLA Ops:
  0.6 144.4 %shard_map.50 = (f32[4,128,32,128]{3,2,1,0:T(8,128)S(1)}, f32[4,32,128]{2,1,0:T(8,128)S(1)}, f32[4,32,128]{2,1,0:T(8,128)S(1)}) custom-call(f32[4,128,32,128]{3,2,1,0:T(8,128)} %tracer.1, f32[4,128,32,128]{3,2,1,0:T(8,128)} %conductance.1, f32[4,128,32,128]{3,2,1,0:T(8,128)} %source.1), custom_call_target="tpu_custom_call" | custom-call | tf_op jit(solution)/shard_map/pallas_call | solution.py:364
  145.0 5.9 %shard_map.51 = (f32[4,128,32,128]{3,2,1,0:T(8,128)}, f32[4,128,32,128]{3,2,1,0:T(8,128)}) custom-call(f32[4,128,32,128]{3,2,1,0:T(8,128)S(1)} %get-tuple-element.5.end, f32[4,32,128]{2,1,0:T(8,128)S(1)} %get-tuple-element.6.mean, f32[4,32,128]{2,1,0:T(8,128)S(1)} %get-tuple-element.7.scale), custom_call_target="tpu_custom_call" | custom-call | tf_op jit(solution)/shard_map/pallas_call | solution.py:403

commit v2 on v1

--- a/solution.py
+++ b/solution.py
@@ -1,4 +1,5 @@
 import functools
+import math
 
 import jax
 import jax.numpy as jnp
@@ -26,6 +27,23 @@
     return 1, J - 2
 
 
+def shares(K):
+    chunks = K // TILE
+    even = chunks // 2
+    return even, max(even, min(even + max(chunks // 4, 1), chunks - 1))
+
+
+def close(total, count):
+    offset = total[0] / count
+    variance = total[1] / count - offset * offset
+    return GUESS + offset, lax.rsqrt(variance + 0.0001)
+
+
+def tally(new, totals):
+    moved = new - GUESS
+    return totals[0] + jnp.sum(moved, axis=0), totals[1] + jnp.sum(moved * moved, axis=0)
+
+
 def when(condition, act):
     if condition is None:
         act()
@@ -34,10 +52,9 @@
 
 
 def kernel(
-    sizes, tracer, conductance, source, end, mean_out, scale_out,
-    even, odd, cond, sour, base, y_halo, z_lower, z_upper, z_first, z_last,
-    sums_early, peer_early, sums_late, peer_late,
-    load_sem, y_send, y_recv, x_send, x_recv, z_send, z_recv, early_send, early_recv, late_send, late_recv,
+    sizes, tracer, conductance, source, end, mean_out, scale_out, base, factor, out_even, out_odd, sums_late,
+    even, odd, cond, sour, y_halo, z_lower, z_upper, z_first, z_last, sums_early, peer_early,
+    load_sem, y_send, y_recv, x_send, x_recv, z_send, z_recv, early_send, early_recv,
 ):
     n_lat, n_lon, n_lev = sizes
     J, I, K, M = tracer.shape
@@ -51,6 +68,8 @@
     field = [even, odd]
     sides = lat_sides(n_lat, lat, J)
     first, number = early_planes(n_lat, lat, J)
+    kept_even, kept_odd = shares(K)
+    odd_lon = lon % 2 == 1
     rows_in = pl.ds(1, I)
 
     def levels(chunk):
@@ -95,12 +114,6 @@
         return pltpu.make_async_remote_copy(
             src_ref=sums_early, dst_ref=peer_early.at[shift - 1],
             send_sem=early_send.at[shift - 1], recv_sem=early_recv.at[shift - 1],
-            device_id={"lon": lax.rem(lon + shift, n_lon)}, device_id_type=MESH)
-
-    def late_copy(chunk, shift):
-        return pltpu.make_async_remote_copy(
-            src_ref=sums_late.at[chunk], dst_ref=peer_late.at[shift - 1, chunk],
-            send_sem=late_send.at[chunk, shift - 1], recv_sem=late_recv.at[chunk, shift - 1],
             device_id={"lon": lax.rem(lon + shift, n_lon)}, device_id_type=MESH)
 
     def sends(axis, way, act):
@@ -208,10 +221,6 @@
 
     zero = jnp.zeros((TILE, M), jnp.float32)
 
-    def tally(new, totals):
-        moved = new - GUESS
-        return totals[0] + jnp.sum(moved, axis=0), totals[1] + jnp.sum(moved * moved, axis=0)
-
     def early_plane(step, chunk, j, inward):
         def body(b, totals):
             r = b * ROWS
@@ -251,6 +260,10 @@
             new = base[s, r, here, :] + cond[plane, r, here, :] * y_halo[step % 2, s, r, here, :]
             if step < STEPS - 1:
                 field[(step + 1) % 2][plane, pl.ds(1 + b * ROWS, ROWS), here, :] = new
+                if step == STEPS - 2 and chunk >= kept_even:
+                    out_even[s, r, levels(chunk - kept_even), :] = new
+                if step == STEPS - 2 and chunk >= kept_odd:
+                    out_odd[s, r, levels(chunk - kept_odd), :] = new
                 return totals
             end[plane, r, here, :] = new
             return tally(new, totals)
@@ -261,6 +274,15 @@
             totals = lax.fori_loop(0, blocks, body, (zero, zero))
             for q in range(2):
                 sums_late[chunk, s, q] = totals[q]
+
+    def stays(step, chunk, act):
+        if step < STEPS - 1 or chunk < kept_even:
+            act()
+        elif chunk < kept_odd:
+            pl.when(odd_lon)(act)
+
+    def y_act(step, chunk, s, act):
+        stays(step, chunk, lambda: when(sides[s][3], act))
 
     loads[-3].wait()
     pack_and_send(0)
@@ -271,85 +293,192 @@
             for way in (0, 1):
                 sends("lon", way, lambda: x_copy(step - 1, way).wait_send())
                 sends("lev", way, lambda: z_copy(step - 1, way).wait_send())
-            for s, side in enumerate(sides):
+            for s in range(len(sides)):
                 for chunk in range(chunks):
-                    when(side[3], lambda: y_copy(step - 1, chunk, s).wait_send())
+                    y_act(step - 1, chunk, s, lambda: y_copy(step - 1, chunk, s).wait_send())
         for way in (0, 1):
             arrives("lon", way, lambda: x_copy(step, way).wait_recv())
             arrives("lev", way, lambda: z_copy(step, way).wait_recv())
         if step == STEPS - 1:
-            for way in (0, 1):
-                sends("lon", way, lambda: x_copy(step, way).wait_send())
-                sends("lev", way, lambda: z_copy(step, way).wait_send())
             for chunk in range(chunks):
                 early_part(step, chunk)
             for shift in range(1, n_lon):
                 early_copy(shift).start()
+            for s, side in enumerate(sides):
+                @pl.loop(0, blocks)
+                def _(b):
+                    rows = pl.ds(b * ROWS, ROWS)
+                    factor[s, rows] = cond[side[0], rows, pl.ds(kept_even * TILE, K - kept_even * TILE), :]
+            for way in (0, 1):
+                sends("lon", way, lambda: x_copy(step, way).wait_send())
+                sends("lev", way, lambda: z_copy(step, way).wait_send())
+            for shift in range(1, n_lon):
+                early_copy(shift).wait_recv()
+
+            @pl.loop(0, number)
+            def _(p):
+                total = [sums_early[p, q] for q in range(2)]
+                for shift in range(1, n_lon):
+                    total = [total[q] + peer_early[shift - 1, p, q] for q in range(2)]
+                mean_out[first + p], scale_out[first + p] = close(total, count)
+
+            for shift in range(1, n_lon):
+                early_copy(shift).wait_send()
         for chunk in range(chunks):
             if step < STEPS - 1:
                 early_part(step, chunk)
-            for s, side in enumerate(sides):
-                when(side[3], lambda: y_arrival(step, chunk, s).wait_recv())
-                late_part(step, chunk, s)
+            for s in range(len(sides)):
+                y_act(step, chunk, s, lambda: y_arrival(step, chunk, s).wait_recv())
+                stays(step, chunk, lambda: late_part(step, chunk, s))
                 if step < STEPS - 1:
-                    when(side[3], lambda: y_copy(step + 1, chunk, s).start())
-            if step == STEPS - 1:
-                for shift in range(1, n_lon):
-                    late_copy(chunk, shift).start()
+                    y_act(step + 1, chunk, s, lambda: y_copy(step + 1, chunk, s).start())
         if step < STEPS - 1:
             pack_and_send(step + 1)
-
-    def close(total):
-        offset = total[0] / count
-        variance = total[1] / count - offset * offset
-        return GUESS + offset, lax.rsqrt(variance + 0.0001)
-
+    for s in range(len(sides)):
+        for chunk in range(chunks):
+            y_act(STEPS - 1, chunk, s, lambda: y_copy(STEPS - 1, chunk, s).wait_send())
+
+
+def finish(
+    sizes, end, base, factor, sums_in, in_even, in_odd, tail, mean_out, scale_out,
+    sums, peer_sums, send_sem, recv_sem,
+):
+    n_lat, n_lon, _ = sizes
+    J, I, K, M = end.shape
+    chunks, blocks = K // TILE, I // ROWS
+    kept_even, kept_odd = shares(K)
+    lat, lon = lax.axis_index("lat"), lax.axis_index("lon")
+    sides = lat_sides(n_lat, lat, J)
+
+    barrier = pltpu.get_barrier_semaphore()
     for shift in range(1, n_lon):
-        early_copy(shift).wait_recv()
-
-    @pl.loop(0, number)
-    def _(p):
-        total = [sums_early[p, q] for q in range(2)]
-        for shift in range(1, n_lon):
-            total = [total[q] + peer_early[shift - 1, p, q] for q in range(2)]
-        mean_out[first + p], scale_out[first + p] = close(total)
-
+        pl.semaphore_signal(barrier, inc=1, device_id={"lon": lax.rem(lon + shift, n_lon)},
+                            device_id_type=MESH)
+
+    def copy(shift):
+        return pltpu.make_async_remote_copy(
+            src_ref=sums, dst_ref=peer_sums.at[shift - 1],
+            send_sem=send_sem.at[shift - 1], recv_sem=recv_sem.at[shift - 1],
+            device_id={"lon": lax.rem(lon + shift, n_lon)}, device_id_type=MESH)
+
+    def levels(chunk):
+        return pl.ds(chunk * TILE, TILE)
+
+    def add(chunk, s, halo, kept):
+        zero = jnp.zeros((TILE, M), jnp.float32)
+
+        def body(b, totals):
+            r = pl.ds(b * ROWS, ROWS)
+            new = base[s, r, levels(chunk), :] + (
+                factor[s, r, levels(chunk - kept_even), :] * halo[s, r, levels(chunk - kept), :])
+            tail[s, r, levels(chunk - kept_even), :] = new
+            return tally(new, totals)
+
+        totals = lax.fori_loop(0, blocks, body, (zero, zero))
+        for q in range(2):
+            sums[chunk, s, q] = totals[q]
+
+    def take(chunk, s):
+        @pl.loop(0, blocks)
+        def _(b):
+            r = pl.ds(b * ROWS, ROWS)
+            tail[s, r, levels(chunk - kept_even), :] = end[sides[s][0], r, levels(chunk), :]
+        for q in range(2):
+            sums[chunk, s, q] = sums_in[chunk, s, q]
+
+    for s in range(len(sides)):
+        for chunk in range(kept_even):
+            for q in range(2):
+                sums[chunk, s, q] = sums_in[chunk, s, q]
+
+        @pl.when(lon % 2 == 0)
+        def _():
+            for chunk in range(kept_even, chunks):
+                add(chunk, s, in_even, kept_even)
+
+        @pl.when(lon % 2 == 1)
+        def _():
+            for chunk in range(kept_even, kept_odd):
+                take(chunk, s)
+            for chunk in range(kept_odd, chunks):
+                add(chunk, s, in_odd, kept_odd)
+
+    pl.semaphore_wait(barrier, n_lon - 1)
     for shift in range(1, n_lon):
-        early_copy(shift).wait_send()
-    for chunk in range(chunks):
-        for s, side in enumerate(sides):
-            when(side[3], lambda: y_copy(STEPS - 1, chunk, s).wait_send())
-    for chunk in range(chunks):
-        for shift in range(1, n_lon):
-            if chunk < chunks - 1:
-                late_copy(chunk, shift).wait_send()
-            late_copy(chunk, shift).wait_recv()
-        for s, side in enumerate(sides):
-            total = [sums_late[chunk, s, q] for q in range(2)]
+        copy(shift).start()
+    for shift in range(1, n_lon):
+        copy(shift).wait_recv()
+    for s in range(len(sides)):
+        for chunk in range(chunks):
+            total = [sums[chunk, s, q] for q in range(2)]
             for shift in range(1, n_lon):
-                total = [total[q] + peer_late[shift - 1, chunk, s, q] for q in range(2)]
-            mean_out[side[0], levels(chunk), :], scale_out[side[0], levels(chunk), :] = close(total)
+                total = [total[q] + peer_sums[shift - 1, chunk, s, q] for q in range(2)]
+            mean_out[s, levels(chunk), :], scale_out[s, levels(chunk), :] = close(total, I * n_lon)
     for shift in range(1, n_lon):
-        late_copy(chunks - 1, shift).wait_send()
-
-
-def write_out(end, mean, scale, standardized, end_out, held, sem):
+        copy(shift).wait_send()
+
+
+def write_early(sizes, end, mean, scale, standardized, end_out, held, sem):
     J, I, K, M = end.shape
-    copies = [pltpu.make_async_copy(end.at[j], end_out.at[j], sem.at[J + j]) for j in range(J)]
-    for copy in copies:
-        copy.start()
-    for j in range(J):
+    first, number = early_planes(sizes[0], lax.axis_index("lat"), J)
+    copies = [pltpu.make_async_copy(
+        end.at[pl.ds(first, number)], end_out.at[pl.ds(first, number)], sem.at[number])]
+    copies[0].start()
+    for p in range(number):
+        j = first + p
         offset, factor = mean[j], scale[j]
 
         @pl.loop(0, I // ROWS)
         def _(b):
             rows = pl.ds(b * ROWS, ROWS)
-            held[j, rows] = (end[j, rows] - offset) * factor
-
-        copies.append(pltpu.make_async_copy(held.at[j], standardized.at[j], sem.at[j]))
+            held[p, rows] = (end[j, rows] - offset) * factor
+
+        copies.append(pltpu.make_async_copy(held.at[p], standardized.at[j], sem.at[p]))
         copies[-1].start()
     for copy in copies:
         copy.wait()
+
+
+def write_late(sizes, end, tail, mean, scale, old_standardized, old_end, standardized, end_out, held, sem):
+    J, I, K, M = end.shape
+    kept = shares(K)[0] * TILE
+    sides = lat_sides(sizes[0], lax.axis_index("lat"), J)
+    pieces = ((end, pl.ds(0, kept)), (tail, pl.ds(kept, K - kept)))
+    copies = []
+    for s, (j, _, _, _, _) in enumerate(sides):
+        sources = (end.at[j, :, pieces[0][1], :], tail.at[s])
+        for n, (_, cut) in enumerate(pieces):
+            copies.append(pltpu.make_async_copy(sources[n], end_out.at[j, :, cut, :], sem.at[s, n]))
+            copies[-1].start()
+    for s, (j, _, _, _, _) in enumerate(sides):
+        for n, (_, cut) in enumerate(pieces):
+            offset, scaling = mean[s, cut, :], scale[s, cut, :]
+
+            @pl.loop(0, I // ROWS)
+            def _(b):
+                rows = pl.ds(b * ROWS, ROWS)
+                new = end[j, rows, cut, :] if n == 0 else tail[s, rows]
+                held[s, rows, cut, :] = (new - offset) * scaling
+
+            copies.append(pltpu.make_async_copy(
+                held.at[s, :, cut, :], standardized.at[j, :, cut, :], sem.at[s, 2 + n]))
+            copies[-1].start()
+    for copy in copies:
+        copy.wait()
+
+
+def cross(sizes, parity, block):
+    n_lat, n_lon, _ = sizes
+
+    def sent(piece, ways):
+        pairs = [(a * n_lon + lon, b * n_lon + lon) for a, b in ways for lon in range(parity, n_lon, 2)]
+        return lax.ppermute(piece, ("lat", "lon"), pairs)
+
+    if n_lat == 2:
+        return sent(block, [(0, 1), (1, 0)])
+    up = sent(block[1:], [(a, a + 1) for a in range(n_lat - 1)])
+    down = sent(block[:1], [(a + 1, a) for a in range(n_lat - 1)])
+    return jnp.concatenate([up, down])
 
 
 def shards(sizes, tracer, conductance, source):
@@ -361,30 +490,30 @@
     peers = max(n_lon - 1, 1)
     late = len(lat_sides(n_lat, 0, J))
     early = early_planes(n_lat, 0, J)[1]
-    end, mean, scale = pl.pallas_call(
+    kept_even, kept_odd = shares(K)
+    hbm, vmem = pl.BlockSpec(memory_space=pltpu.HBM), pl.BlockSpec(memory_space=pltpu.VMEM)
+    out_of = (late, I, K - kept_even * TILE, M)
+    scratch = [
+        (J, I + 2, K, M), (J, I + 2, K, M), (J, I, K, M), (J, I, K, M), (2, late, I, K, M),
+        (2, J, I, 1, M), (2, J, I, 1, M), (2, J, I, 1, M), (2, J, I, 1, M),
+        (early, 2, K, M), (peers, early, 2, K, M),
+    ]
+    limit = sum(4 * math.prod(shape) for shape in scratch) + (2 << 20)
+    end, mean, scale, base, factor, out_even, out_odd, sums = pl.pallas_call(
         functools.partial(kernel, sizes),
         out_shape=[
             pltpu.VMEM((J, I, K, M), f32),
             pltpu.VMEM((J, K, M), f32),
             pltpu.VMEM((J, K, M), f32),
+            pltpu.VMEM((late, I, K, M), f32),
+            pltpu.VMEM(out_of, f32),
+            pltpu.VMEM(out_of, f32),
+            pltpu.VMEM((late, I, K - kept_odd * TILE, M), f32),
+            pltpu.VMEM((chunks, late, 2, TILE, M), f32),
         ],
-        in_specs=[pl.BlockSpec(memory_space=pltpu.HBM)] * 3,
-        out_specs=[pl.BlockSpec(memory_space=pltpu.VMEM)] * 3,
-        scratch_shapes=[
-            pltpu.VMEM((J, I + 2, K, M), f32),
-            pltpu.VMEM((J, I + 2, K, M), f32),
-            pltpu.VMEM((J, I, K, M), f32),
-            pltpu.VMEM((J, I, K, M), f32),
-            pltpu.VMEM((late, I, K, M), f32),
-            pltpu.VMEM((2, late, I, K, M), f32),
-            pltpu.VMEM((2, J, I, 1, M), f32),
-            pltpu.VMEM((2, J, I, 1, M), f32),
-            pltpu.VMEM((2, J, I, 1, M), f32),
-            pltpu.VMEM((2, J, I, 1, M), f32),
-            pltpu.VMEM((early, 2, K, M), f32),
-            pltpu.VMEM((peers, early, 2, K, M), f32),
-            pltpu.VMEM((chunks, late, 2, TILE, M), f32),
-            pltpu.VMEM((peers, chunks, late, 2, TILE, M), f32),
+        in_specs=[hbm] * 3,
+        out_specs=[vmem] * 8,
+        scratch_shapes=[pltpu.VMEM(shape, f32) for shape in scratch] + [
             dma((3 + late,)),
             dma((STEPS, chunks, late)),
             dma((STEPS, chunks, late)),
@@ -394,20 +523,47 @@
             dma((STEPS, 2)),
             dma((peers,)),
             dma((peers,)),
-            dma((chunks, peers)),
-            dma((chunks, peers)),
         ],
         compiler_params=pltpu.CompilerParams(
-            collective_id=0, has_side_effects=True, vmem_limit_bytes=50 * 1024 * 1024),
+            collective_id=0, has_side_effects=True, vmem_limit_bytes=limit),
     )(tracer, conductance, source)
+    in_even = cross(sizes, 0, out_even)
+    in_odd = cross(sizes, 1, out_odd)
+    whole = jax.ShapeDtypeStruct((J, I, K, M), f32)
+    standardized, end_out = pl.pallas_call(
+        functools.partial(write_early, sizes),
+        out_shape=[whole] * 2,
+        in_specs=[vmem] * 3,
+        out_specs=[hbm] * 2,
+        scratch_shapes=[pltpu.VMEM((early, I, K, M), f32), dma((early + 1,))],
+        compiler_params=pltpu.CompilerParams(vmem_limit_bytes=16 << 20),
+        cost_estimate=pl.CostEstimate(
+            flops=1 << 32, bytes_accessed=8 * early * I * K * M, transcendentals=0),
+    )(end, mean, scale)
+    tail, mean, scale = pl.pallas_call(
+        functools.partial(finish, sizes),
+        out_shape=[
+            pltpu.VMEM(out_of, f32), pltpu.VMEM((late, K, M), f32), pltpu.VMEM((late, K, M), f32)],
+        in_specs=[vmem] * 6,
+        out_specs=[vmem] * 3,
+        scratch_shapes=[
+            pltpu.VMEM((chunks, late, 2, TILE, M), f32),
+            pltpu.VMEM((peers, chunks, late, 2, TILE, M), f32),
+            dma((peers,)),
+            dma((peers,)),
+        ],
+        compiler_params=pltpu.CompilerParams(
+            collective_id=1, has_side_effects=True, vmem_limit_bytes=4 << 20),
+    )(end, base, factor, sums, in_even, in_odd)
     return pl.pallas_call(
-        write_out,
-        out_shape=[jax.ShapeDtypeStruct((J, I, K, M), f32)] * 2,
-        in_specs=[pl.BlockSpec(memory_space=pltpu.VMEM)] * 3,
-        out_specs=[pl.BlockSpec(memory_space=pltpu.HBM)] * 2,
-        scratch_shapes=[pltpu.VMEM((J, I, K, M), f32), dma((2 * J,))],
-        compiler_params=pltpu.CompilerParams(vmem_limit_bytes=32 * 1024 * 1024),
-    )(end, mean, scale)
+        functools.partial(write_late, sizes),
+        out_shape=[whole] * 2,
+        in_specs=[vmem] * 4 + [hbm] * 2,
+        out_specs=[hbm] * 2,
+        input_output_aliases={4: 0, 5: 1},
+        scratch_shapes=[pltpu.VMEM((late, I, K, M), f32), dma((late, 4))],
+        compiler_params=pltpu.CompilerParams(vmem_limit_bytes=8 << 20),
+    )(end, tail, mean, scale, standardized, end_out)
 
 
 def solution(mesh):

time: 151 us -> 149 us (0.987)
  Pallas kernels: 150 us -> 130 us
  waiting for transfers between devices: 0 us -> 14.5 us
  starting transfers between devices: 0 us -> 3.06 us
    pallas_call x1, Pallas kernels: 144 us -> 119 us  [shards(): pl.pallas_call(functools.partial(kernel, sizes), out_shape=[pltpu.VMEM((J...]
    ppermute x0 -> x2, waiting for transfers between devices: none -> 14.5 us  [sent(): return lax.ppermute(piece, ('lat', 'lon'), pairs)]
    pallas_call x1 -> x3, Pallas kernels: 5.92 us -> 10.9 us  [the longest x1 4.7 us: shards(): pl.pallas_call(functools.partial(write_early, sizes), out_shape=[whole] *...]
    ppermute x0 -> x2, starting transfers between devices: none -> 3.06 us  [sent(): return lax.ppermute(piece, ('lat', 'lon'), pairs)]
  transfers between devices with their start and end apart: 0 -> 2, of which waited for: 0 -> 1; matrix products, arithmetic and copies ran while one was open for 0% -> 0% of each run, Pallas kernels for 0% -> 3%
where the time goes in v2:
time: 149 us
  Pallas kernels  130 us (87%)
  waiting for transfers between devices  14.5 us (10%)
  starting transfers between devices  3.06 us (2%)
    pallas_call x1, Pallas kernels, shards(): pl.pallas_call(functools.partial(kernel, sizes), out_shape=[pltpu.VMEM((J...  119 us
    ppermute x2, waiting for transfers between devices, sent(): return lax.ppermute(piece, ('lat', 'lon'), pairs)  14.5 us
    pallas_call x1, Pallas kernels, shards(): pl.pallas_call(functools.partial(write_early, sizes), out_shape=[whole] *...  4.7 us
    pallas_call x1, Pallas kernels, shards(): pl.pallas_call(functools.partial(finish, sizes), out_shape=[pltpu.VMEM(ou...  4.12 us
    ppermute x2, starting transfers between devices, sent(): return lax.ppermute(piece, ('lat', 'lon'), pairs)  3.06 us
  transfers between devices with their start and end apart: 2, of which 1 were waited for; matrix products, arithmetic and copies ran while one was open for 0% of the time, Pallas kernels for 3%

profile of v2, /device:TPU:0, one launch (start us, length us, event | category | flops | bytes accessed | tf_op | source)
XLA Modules:
  0.0 148.6 jit_solution(8079229924633915131)
XLA Ops:
  0.6 119.4 %shard_map.50 = (f32[4,128,32,128]{3,2,1,0:T(8,128)S(1)}, f32[4,32,128]{2,1,0:T(8,128)S(1)}, f32[4,32,128]{2,1,0:T(8,128)S(1)}, f32[1,128,32,128]{3,2,1,0:T(8,12...) custom-call(f32[4,128,32,128]{3,2,1,0:T(8,128)} %tracer.1, ...), custom_call_target="tpu_custom_call" | custom-call | tf_op jit(solution)/shard_map/pallas_call | solution.py:502
  120.1 2.4 %collective-permute-start = (f32[1,128,16,128]{3,2,1,0:T(8,128)S(1)}, f32[1,128,16,128]{3,2,1,0:T(8,128)S(1)}, u32[]{:S(2)}, u32[]{:S(2)}) collective-permute-start(f32[1,128,16,128]{3,2,1,0:T(8,128)S(1)} %get-tuple-element.19), channel_id=1, source_target_pairs={{0,16},{8,24},{16,0},{24,8},{1,17},{9,25},{17,1},{25,9},{2,18},{10... | collective-permute-start | bytes 3145736 | tf_op jit(solution)/shard_map/ppermute | solution.py:475
  122.4 0.7 collective-permute-start.1
  123.1 4.7 %shard_map.52 = (f32[4,128,32,128]{3,2,1,0:T(8,128)}, f32[4,128,32,128]{3,2,1,0:T(8,128)}) custom-call(f32[4,128,32,128]{3,2,1,0:T(8,128)S(1)} %get-tuple-element.15.end, f32[4,32,128]{2,1,0:T(8,128)S(1)} %get-tuple-element.24.mean, f32[4,32,128]{2,1,0:T(8,128)S(1)} %get-tuple-element.25.scale), custom_call_target="tpu_custom_call" | custom-call | flops 4294967296 | bytes 12582912 | tf_op jit(solution)/shard_map/pallas_call | solution.py:533
  127.8 0.0 collective-permute-done.1.in_odd
  127.9 14.5 %collective-permute-done.in_even = f32[1,128,16,128]{3,2,1,0:T(8,128)S(1)} collective-permute-done((f32[1,128,16,128]{3,2,1,0:T(8,128)S(1)}, f32[1,128,16,128]{3,2,1,0:T(8,128)S(1)}, u32[]{:S(2)}, u32[]{:S(2)}) %collective-permute-start) | collective-permute-done | bytes 1048608 | tf_op jit(solution)/shard_map/ppermute | solution.py:475
  142.4 4.1 %shard_map.51 = (f32[1,128,16,128]{3,2,1,0:T(8,128)S(1)}, f32[1,32,128]{2,1,0:T(8,128)S(1)}, f32[1,32,128]{2,1,0:T(8,128)S(1)}) custom-call(f32[4,128,32,128]{3,2,1,0:T(8,128)S(1)} %get-tuple-element.15.end, f32[1,128,32,128]{3,2,1,0:T(8,128)S(1)} %get-tuple-element.16.base, f32[1,128,16,128]{3,2,1,0:T(8,128)S(1)} %get-tuple-element.17.factor, ...), custom_call_target="tpu_custom_call" | custom-call | tf_op jit(solution)/shard_map/pallas_call | solution.py:543
  146.5 2.1 %shard_map.53 = (f32[4,128,32,128]{3,2,1,0:T(8,128)}, f32[4,128,32,128]{3,2,1,0:T(8,128)}) custom-call(f32[4,128,32,128]{3,2,1,0:T(8,128)S(1)} %get-tuple-element.15.end, f32[1,128,16,128]{3,2,1,0:T(8,128)S(1)} %get-tuple-element.21.tail, f32[1,32,128]{2,1,0:T(8,128)S(1)} %get-tuple-element.22.mean, ...), custom_call_target="tpu_custom_call", output_to_operand_aliasing={{0}: (4, {}), {1}: (5, {})} | custom-call | tf_op jit(solution)/shard_map/pallas_call | solution.py:558
Async XLA Ops:
  120.1 22.3 %collective-permute-start = (f32[1,128,16,128]{3,2,1,0:T(8,128)S(1)}, f32[1,128,16,128]{3,2,1,0:T(8,128)S(1)}, u32[]{:S(2)}, u32[]{:S(2)}) collective-permute-start(f32[1,128,16,128]{3,2,1,0:T(8,128)S(1)} %get-tuple-element.19), channel_id=1, source_target_pairs={{0,16},{8,24},{16,0},{24,8},{1,17},{9,25},{17,1},{25,9},{2,18},{10... | collective-permute-start | bytes 3145736 | tf_op jit(solution)/shard_map/ppermute | solution.py:475
  122.4 5.4 %collective-permute-start.1 = (f32[1,128,8,128]{3,2,1,0:T(8,128)S(1)}, f32[1,128,8,128]{3,2,1,0:T(8,128)S(1)}, u32[]{:S(2)}, u32[]{:S(2)}) collective-permute-start(f32[1,128,8,128]{3,2,1,0:T(8,128)S(1)} %get-tuple-element.20), channel_id=1, source_target_pairs={{4,20},{12,28},{20,4},{28,12},{5,21},{13,29},{21,5},{29,13},{6,22}... | collective-permute-start | bytes 1572872 | tf_op jit(solution)/shard_map/ppermute | solution.py:475

commit v3 on v2

--- a/solution.py
+++ b/solution.py
@@ -27,10 +27,8 @@
     return 1, J - 2
 
 
-def shares(K):
-    chunks = K // TILE
-    even = chunks // 2
-    return even, max(even, min(even + max(chunks // 4, 1), chunks - 1))
+def kept(K):
+    return K // TILE // 2
 
 
 def close(total, count):
@@ -52,7 +50,7 @@
 
 
 def kernel(
-    sizes, tracer, conductance, source, end, mean_out, scale_out, base, factor, out_even, out_odd, sums_late,
+    sizes, tracer, conductance, source, end, mean_out, scale_out, base, factor, out, sums_late,
     even, odd, cond, sour, y_halo, z_lower, z_upper, z_first, z_last, sums_early, peer_early,
     load_sem, y_send, y_recv, x_send, x_recv, z_send, z_recv, early_send, early_recv,
 ):
@@ -68,7 +66,7 @@
     field = [even, odd]
     sides = lat_sides(n_lat, lat, J)
     first, number = early_planes(n_lat, lat, J)
-    kept_even, kept_odd = shares(K)
+    stay = kept(K)
     odd_lon = lon % 2 == 1
     rows_in = pl.ds(1, I)
 
@@ -94,20 +92,22 @@
             send_sem=y_send.at[step, chunk, s], recv_sem=y_recv.at[step, chunk, s],
             device_id={"lat": peer}, device_id_type=MESH)
 
-    def x_copy(step, way):
+    faces = [pl.ds(first, number)] + [pl.ds(side[0], 1) for side in sides]
+
+    def x_copy(step, way, part):
         buf = field[step % 2]
         return pltpu.make_async_remote_copy(
-            src_ref=buf.at[:, I if way == 0 else 1],
-            dst_ref=buf.at[:, 0 if way == 0 else I + 1],
-            send_sem=x_send.at[step, way], recv_sem=x_recv.at[step, way],
+            src_ref=buf.at[faces[part], I if way == 0 else 1],
+            dst_ref=buf.at[faces[part], 0 if way == 0 else I + 1],
+            send_sem=x_send.at[step, way, part], recv_sem=x_recv.at[step, way, part],
             device_id=target("lon", way), device_id_type=MESH)
 
-    def z_copy(step, way):
+    def z_copy(step, way, part):
         src = z_last if way == 0 else z_first
         dst = z_lower if way == 0 else z_upper
         return pltpu.make_async_remote_copy(
-            src_ref=src.at[step % 2], dst_ref=dst.at[step % 2],
-            send_sem=z_send.at[step, way], recv_sem=z_recv.at[step, way],
+            src_ref=src.at[step % 2, faces[part]], dst_ref=dst.at[step % 2, faces[part]],
+            send_sem=z_send.at[step, way, part], recv_sem=z_recv.at[step, way, part],
             device_id=target("lev", way), device_id_type=MESH)
 
     def early_copy(shift):
@@ -180,19 +180,31 @@
                             jnp.zeros((ROWS, 1, M), jnp.float32))
         pl.when(jnp.logical_not((below if way == 0 else above)["lev"]))(no_z)
 
-    def pack_and_send(step):
+    def pack_and_send(step, part):
         buf = field[step % 2]
+        start, extent = (first, number) if part == 0 else (sides[part - 1][0], 1)
         for way in (0, 1):
-            sends("lon", way, lambda: x_copy(step, way).start())
-
-        @pl.loop(0, J * blocks)
+            sends("lon", way, lambda: x_copy(step, way, part).start())
+
+        @pl.loop(0, extent * blocks)
         def _(q):
-            j, r = q // blocks, (q % blocks) * ROWS
+            j, r = start + q // blocks, (q % blocks) * ROWS
             z_first[step % 2, j, pl.ds(r, ROWS)] = buf[j, pl.ds(1 + r, ROWS), pl.ds(0, 1), :]
             z_last[step % 2, j, pl.ds(r, ROWS)] = buf[j, pl.ds(1 + r, ROWS), pl.ds(K - 1, 1), :]
 
         for way in (0, 1):
-            sends("lev", way, lambda: z_copy(step, way).start())
+            sends("lev", way, lambda: z_copy(step, way, part).start())
+
+    def faces_sent(step):
+        for part in range(len(faces)):
+            for way in (0, 1):
+                sends("lon", way, lambda: x_copy(step, way, part).wait_send())
+                sends("lev", way, lambda: z_copy(step, way, part).wait_send())
+
+    def faces_arrive(step, part):
+        for way in (0, 1):
+            arrives("lon", way, lambda: x_copy(step, way, part).wait_recv())
+            arrives("lev", way, lambda: z_copy(step, way, part).wait_recv())
 
     def next_rows(step, chunk, j, r, inward):
         buf = field[step % 2]
@@ -245,6 +257,8 @@
 
         if n_lat == 2:
             early_plane(step, chunk, jnp.where(lat == 0, 0, J - 1), jnp.where(lat == 0, 1, J - 2))
+
+    def base_part(step, chunk):
         for s, (plane, inward, _, _, _) in enumerate(sides):
             @pl.loop(0, blocks)
             def _(b):
@@ -260,10 +274,8 @@
             new = base[s, r, here, :] + cond[plane, r, here, :] * y_halo[step % 2, s, r, here, :]
             if step < STEPS - 1:
                 field[(step + 1) % 2][plane, pl.ds(1 + b * ROWS, ROWS), here, :] = new
-                if step == STEPS - 2 and chunk >= kept_even:
-                    out_even[s, r, levels(chunk - kept_even), :] = new
-                if step == STEPS - 2 and chunk >= kept_odd:
-                    out_odd[s, r, levels(chunk - kept_odd), :] = new
+                if step == STEPS - 2 and chunk >= stay:
+                    out[s, r, levels(chunk - stay), :] = new
                 return totals
             end[plane, r, here, :] = new
             return tally(new, totals)
@@ -275,43 +287,48 @@
             for q in range(2):
                 sums_late[chunk, s, q] = totals[q]
 
-    def stays(step, chunk, act):
-        if step < STEPS - 1 or chunk < kept_even:
-            act()
-        elif chunk < kept_odd:
-            pl.when(odd_lon)(act)
-
-    def y_act(step, chunk, s, act):
-        stays(step, chunk, lambda: when(sides[s][3], act))
+    def y_start(step, chunk, s, condition=None):
+        exists = sides[s][3]
+        if condition is not None and exists is not None:
+            condition = jnp.logical_and(condition, exists)
+        when(exists if condition is None else condition, lambda: y_copy(step, chunk, s).start())
 
     loads[-3].wait()
-    pack_and_send(0)
+    for part in range(len(faces)):
+        pack_and_send(0, part)
     loads[-2].wait()
     loads[-1].wait()
     for step in range(STEPS):
+        last = step == STEPS - 1
         if step >= 1:
-            for way in (0, 1):
-                sends("lon", way, lambda: x_copy(step - 1, way).wait_send())
-                sends("lev", way, lambda: z_copy(step - 1, way).wait_send())
-            for s in range(len(sides)):
-                for chunk in range(chunks):
-                    y_act(step - 1, chunk, s, lambda: y_copy(step - 1, chunk, s).wait_send())
-        for way in (0, 1):
-            arrives("lon", way, lambda: x_copy(step, way).wait_recv())
-            arrives("lev", way, lambda: z_copy(step, way).wait_recv())
-        if step == STEPS - 1:
-            for chunk in range(chunks):
-                early_part(step, chunk)
+            faces_sent(step - 1)
+        faces_arrive(step, 0)
+        for chunk in range(chunks):
+            early_part(step, chunk)
+            if last and chunk == max(chunks - 2, 0):
+                for held in range(stay):
+                    for s in range(len(sides)):
+                        y_start(step, held, s, odd_lon)
+        if last:
             for shift in range(1, n_lon):
                 early_copy(shift).start()
+        else:
+            pack_and_send(step + 1, 0)
+        for part in range(1, len(faces)):
+            faces_arrive(step, part)
+        for chunk in range(chunks):
+            base_part(step, chunk)
+        if step >= 1:
+            for s, side in enumerate(sides):
+                for chunk in range(chunks):
+                    when(side[3], lambda: y_copy(step - 1, chunk, s).wait_send())
+        if last:
             for s, side in enumerate(sides):
                 @pl.loop(0, blocks)
                 def _(b):
                     rows = pl.ds(b * ROWS, ROWS)
-                    factor[s, rows] = cond[side[0], rows, pl.ds(kept_even * TILE, K - kept_even * TILE), :]
-            for way in (0, 1):
-                sends("lon", way, lambda: x_copy(step, way).wait_send())
-                sends("lev", way, lambda: z_copy(step, way).wait_send())
+                    factor[s, rows] = cond[side[0], rows, pl.ds(stay * TILE, K - stay * TILE), :]
+            faces_sent(step)
             for shift in range(1, n_lon):
                 early_copy(shift).wait_recv()
 
@@ -324,31 +341,29 @@
 
             for shift in range(1, n_lon):
                 early_copy(shift).wait_send()
-        for chunk in range(chunks):
-            if step < STEPS - 1:
-                early_part(step, chunk)
-            for s in range(len(sides)):
-                y_act(step, chunk, s, lambda: y_arrival(step, chunk, s).wait_recv())
-                stays(step, chunk, lambda: late_part(step, chunk, s))
-                if step < STEPS - 1:
-                    y_act(step + 1, chunk, s, lambda: y_copy(step + 1, chunk, s).start())
-        if step < STEPS - 1:
-            pack_and_send(step + 1)
-    for s in range(len(sides)):
-        for chunk in range(chunks):
-            y_act(STEPS - 1, chunk, s, lambda: y_copy(STEPS - 1, chunk, s).wait_send())
+        for chunk in range(stay if last else chunks):
+            for s, side in enumerate(sides):
+                when(side[3], lambda: y_arrival(step, chunk, s).wait_recv())
+                late_part(step, chunk, s)
+                if step < STEPS - 2:
+                    y_start(step + 1, chunk, s)
+                elif not last and chunk < stay:
+                    y_start(step + 1, chunk, s, jnp.logical_not(odd_lon))
+        if not last:
+            for part in range(1, len(faces)):
+                pack_and_send(step + 1, part)
+    for s, side in enumerate(sides):
+        for chunk in range(stay):
+            when(side[3], lambda: y_copy(STEPS - 1, chunk, s).wait_send())
 
 
 def finish(
-    sizes, end, base, factor, sums_in, in_even, in_odd, tail, mean_out, scale_out,
-    sums, peer_sums, send_sem, recv_sem,
+    sizes, base, factor, sums_in, halo, tail, mean_out, scale_out, sums, peer_sums, send_sem, recv_sem,
 ):
     n_lat, n_lon, _ = sizes
-    J, I, K, M = end.shape
-    chunks, blocks = K // TILE, I // ROWS
-    kept_even, kept_odd = shares(K)
-    lat, lon = lax.axis_index("lat"), lax.axis_index("lon")
-    sides = lat_sides(n_lat, lat, J)
+    late, I, K, M = base.shape
+    chunks, blocks, stay = K // TILE, I // ROWS, kept(K)
+    lon = lax.axis_index("lon")
 
     barrier = pltpu.get_barrier_semaphore()
     for shift in range(1, n_lon):
@@ -361,69 +376,52 @@
             send_sem=send_sem.at[shift - 1], recv_sem=recv_sem.at[shift - 1],
             device_id={"lon": lax.rem(lon + shift, n_lon)}, device_id_type=MESH)
 
-    def levels(chunk):
-        return pl.ds(chunk * TILE, TILE)
-
-    def add(chunk, s, halo, kept):
-        zero = jnp.zeros((TILE, M), jnp.float32)
-
-        def body(b, totals):
-            r = pl.ds(b * ROWS, ROWS)
-            new = base[s, r, levels(chunk), :] + (
-                factor[s, r, levels(chunk - kept_even), :] * halo[s, r, levels(chunk - kept), :])
-            tail[s, r, levels(chunk - kept_even), :] = new
-            return tally(new, totals)
-
-        totals = lax.fori_loop(0, blocks, body, (zero, zero))
-        for q in range(2):
-            sums[chunk, s, q] = totals[q]
-
-    def take(chunk, s):
-        @pl.loop(0, blocks)
-        def _(b):
-            r = pl.ds(b * ROWS, ROWS)
-            tail[s, r, levels(chunk - kept_even), :] = end[sides[s][0], r, levels(chunk), :]
-        for q in range(2):
-            sums[chunk, s, q] = sums_in[chunk, s, q]
-
-    for s in range(len(sides)):
-        for chunk in range(kept_even):
+    zero = jnp.zeros((TILE, M), jnp.float32)
+    for s in range(late):
+        for chunk in range(stay):
             for q in range(2):
                 sums[chunk, s, q] = sums_in[chunk, s, q]
-
-        @pl.when(lon % 2 == 0)
-        def _():
-            for chunk in range(kept_even, chunks):
-                add(chunk, s, in_even, kept_even)
-
-        @pl.when(lon % 2 == 1)
-        def _():
-            for chunk in range(kept_even, kept_odd):
-                take(chunk, s)
-            for chunk in range(kept_odd, chunks):
-                add(chunk, s, in_odd, kept_odd)
+        for chunk in range(stay, chunks):
+            here, there = pl.ds(chunk * TILE, TILE), pl.ds((chunk - stay) * TILE, TILE)
+
+            def body(b, totals):
+                r = pl.ds(b * ROWS, ROWS)
+                new = base[s, r, here, :] + factor[s, r, there, :] * halo[s, r, there, :]
+                tail[s, r, there, :] = new
+                return tally(new, totals)
+
+            totals = lax.fori_loop(0, blocks, body, (zero, zero))
+            for q in range(2):
+                sums[chunk, s, q] = totals[q]
 
     pl.semaphore_wait(barrier, n_lon - 1)
     for shift in range(1, n_lon):
         copy(shift).start()
     for shift in range(1, n_lon):
         copy(shift).wait_recv()
-    for s in range(len(sides)):
+    for s in range(late):
         for chunk in range(chunks):
             total = [sums[chunk, s, q] for q in range(2)]
             for shift in range(1, n_lon):
                 total = [total[q] + peer_sums[shift - 1, chunk, s, q] for q in range(2)]
-            mean_out[s, levels(chunk), :], scale_out[s, levels(chunk), :] = close(total, I * n_lon)
+            here = pl.ds(chunk * TILE, TILE)
+            mean_out[s, here, :], scale_out[s, here, :] = close(total, I * n_lon)
     for shift in range(1, n_lon):
         copy(shift).wait_send()
 
 
 def write_early(sizes, end, mean, scale, standardized, end_out, held, sem):
     J, I, K, M = end.shape
-    first, number = early_planes(sizes[0], lax.axis_index("lat"), J)
+    lat = lax.axis_index("lat")
+    first, number = early_planes(sizes[0], lat, J)
+    done = pl.ds(0, kept(K) * TILE)
     copies = [pltpu.make_async_copy(
         end.at[pl.ds(first, number)], end_out.at[pl.ds(first, number)], sem.at[number])]
-    copies[0].start()
+    for s, side in enumerate(lat_sides(sizes[0], lat, J)):
+        copies.append(pltpu.make_async_copy(
+            end.at[side[0], :, done, :], end_out.at[side[0], :, done, :], sem.at[number + 1 + s]))
+    for copy in copies:
+        copy.start()
     for p in range(number):
         j = first + p
         offset, factor = mean[j], scale[j]
@@ -441,43 +439,35 @@
 
 def write_late(sizes, end, tail, mean, scale, old_standardized, old_end, standardized, end_out, held, sem):
     J, I, K, M = end.shape
-    kept = shares(K)[0] * TILE
-    sides = lat_sides(sizes[0], lax.axis_index("lat"), J)
-    pieces = ((end, pl.ds(0, kept)), (tail, pl.ds(kept, K - kept)))
+    cut = kept(K) * TILE
+    low, high = pl.ds(0, cut), pl.ds(cut, K - cut)
     copies = []
-    for s, (j, _, _, _, _) in enumerate(sides):
-        sources = (end.at[j, :, pieces[0][1], :], tail.at[s])
-        for n, (_, cut) in enumerate(pieces):
-            copies.append(pltpu.make_async_copy(sources[n], end_out.at[j, :, cut, :], sem.at[s, n]))
-            copies[-1].start()
-    for s, (j, _, _, _, _) in enumerate(sides):
-        for n, (_, cut) in enumerate(pieces):
-            offset, scaling = mean[s, cut, :], scale[s, cut, :]
+    for s, side in enumerate(lat_sides(sizes[0], lax.axis_index("lat"), J)):
+        j = side[0]
+        copies.append(pltpu.make_async_copy(tail.at[s], end_out.at[j, :, high, :], sem.at[s, 0]))
+        copies[-1].start()
+        for n, here in enumerate((low, high)):
+            offset, scaling = mean[s, here, :], scale[s, here, :]
 
             @pl.loop(0, I // ROWS)
             def _(b):
                 rows = pl.ds(b * ROWS, ROWS)
-                new = end[j, rows, cut, :] if n == 0 else tail[s, rows]
-                held[s, rows, cut, :] = (new - offset) * scaling
+                new = end[j, rows, here, :] if n == 0 else tail[s, rows]
+                held[s, rows, here, :] = (new - offset) * scaling
 
             copies.append(pltpu.make_async_copy(
-                held.at[s, :, cut, :], standardized.at[j, :, cut, :], sem.at[s, 2 + n]))
+                held.at[s, :, here, :], standardized.at[j, :, here, :], sem.at[s, 1 + n]))
             copies[-1].start()
     for copy in copies:
         copy.wait()
 
 
-def cross(sizes, parity, block):
-    n_lat, n_lon, _ = sizes
-
-    def sent(piece, ways):
-        pairs = [(a * n_lon + lon, b * n_lon + lon) for a, b in ways for lon in range(parity, n_lon, 2)]
-        return lax.ppermute(piece, ("lat", "lon"), pairs)
-
+def cross(sizes, block):
+    n_lat = sizes[0]
     if n_lat == 2:
-        return sent(block, [(0, 1), (1, 0)])
-    up = sent(block[1:], [(a, a + 1) for a in range(n_lat - 1)])
-    down = sent(block[:1], [(a + 1, a) for a in range(n_lat - 1)])
+        return lax.ppermute(block, "lat", [(0, 1), (1, 0)])
+    up = lax.ppermute(block[1:], "lat", [(a, a + 1) for a in range(n_lat - 1)])
+    down = lax.ppermute(block[:1], "lat", [(a + 1, a) for a in range(n_lat - 1)])
     return jnp.concatenate([up, down])
 
 
@@ -490,16 +480,16 @@
     peers = max(n_lon - 1, 1)
     late = len(lat_sides(n_lat, 0, J))
     early = early_planes(n_lat, 0, J)[1]
-    kept_even, kept_odd = shares(K)
+    stay = kept(K)
     hbm, vmem = pl.BlockSpec(memory_space=pltpu.HBM), pl.BlockSpec(memory_space=pltpu.VMEM)
-    out_of = (late, I, K - kept_even * TILE, M)
+    out_of = (late, I, K - stay * TILE, M)
     scratch = [
         (J, I + 2, K, M), (J, I + 2, K, M), (J, I, K, M), (J, I, K, M), (2, late, I, K, M),
         (2, J, I, 1, M), (2, J, I, 1, M), (2, J, I, 1, M), (2, J, I, 1, M),
         (early, 2, K, M), (peers, early, 2, K, M),
     ]
     limit = sum(4 * math.prod(shape) for shape in scratch) + (2 << 20)
-    end, mean, scale, base, factor, out_even, out_odd, sums = pl.pallas_call(
+    end, mean, scale, base, factor, out, sums = pl.pallas_call(
         functools.partial(kernel, sizes),
         out_shape=[
             pltpu.VMEM((J, I, K, M), f32),
@@ -508,34 +498,32 @@
             pltpu.VMEM((late, I, K, M), f32),
             pltpu.VMEM(out_of, f32),
             pltpu.VMEM(out_of, f32),
-            pltpu.VMEM((late, I, K - kept_odd * TILE, M), f32),
             pltpu.VMEM((chunks, late, 2, TILE, M), f32),
         ],
         in_specs=[hbm] * 3,
-        out_specs=[vmem] * 8,
+        out_specs=[vmem] * 7,
         scratch_shapes=[pltpu.VMEM(shape, f32) for shape in scratch] + [
             dma((3 + late,)),
             dma((STEPS, chunks, late)),
             dma((STEPS, chunks, late)),
-            dma((STEPS, 2)),
-            dma((STEPS, 2)),
-            dma((STEPS, 2)),
-            dma((STEPS, 2)),
+            dma((STEPS, 2, 1 + late)),
+            dma((STEPS, 2, 1 + late)),
+            dma((STEPS, 2, 1 + late)),
+            dma((STEPS, 2, 1 + late)),
             dma((peers,)),
             dma((peers,)),
         ],
         compiler_params=pltpu.CompilerParams(
             collective_id=0, has_side_effects=True, vmem_limit_bytes=limit),
     )(tracer, conductance, source)
-    in_even = cross(sizes, 0, out_even)
-    in_odd = cross(sizes, 1, out_odd)
+    halo = cross(sizes, out)
     whole = jax.ShapeDtypeStruct((J, I, K, M), f32)
     standardized, end_out = pl.pallas_call(
         functools.partial(write_early, sizes),
         out_shape=[whole] * 2,
         in_specs=[vmem] * 3,
         out_specs=[hbm] * 2,
-        scratch_shapes=[pltpu.VMEM((early, I, K, M), f32), dma((early + 1,))],
+        scratch_shapes=[pltpu.VMEM((early, I, K, M), f32), dma((early + 1 + late,))],
         compiler_params=pltpu.CompilerParams(vmem_limit_bytes=16 << 20),
         cost_estimate=pl.CostEstimate(
             flops=1 << 32, bytes_accessed=8 * early * I * K * M, transcendentals=0),
@@ -544,7 +532,7 @@
         functools.partial(finish, sizes),
         out_shape=[
             pltpu.VMEM(out_of, f32), pltpu.VMEM((late, K, M), f32), pltpu.VMEM((late, K, M), f32)],
-        in_specs=[vmem] * 6,
+        in_specs=[vmem] * 4,
         out_specs=[vmem] * 3,
         scratch_shapes=[
             pltpu.VMEM((chunks, late, 2, TILE, M), f32),
@@ -554,14 +542,14 @@
         ],
         compiler_params=pltpu.CompilerParams(
             collective_id=1, has_side_effects=True, vmem_limit_bytes=4 << 20),
-    )(end, base, factor, sums, in_even, in_odd)
+    )(base, factor, sums, halo)
     return pl.pallas_call(
         functools.partial(write_late, sizes),
         out_shape=[whole] * 2,
         in_specs=[vmem] * 4 + [hbm] * 2,
         out_specs=[hbm] * 2,
         input_output_aliases={4: 0, 5: 1},
-        scratch_shapes=[pltpu.VMEM((late, I, K, M), f32), dma((late, 4))],
+        scratch_shapes=[pltpu.VMEM((late, I, K, M), f32), dma((late, 3))],
         compiler_params=pltpu.CompilerParams(vmem_limit_bytes=8 << 20),
     )(end, tail, mean, scale, standardized, end_out)
 

time: 149 us -> 147 us (0.987)
  starting transfers between devices: 3.06 us -> 0.07 us
  waiting for transfers between devices: 14.5 us -> 17.1 us
  Pallas kernels: 130 us -> 128 us
    pallas_call x1, Pallas kernels: 119 us -> 113 us  [shards(): pl.pallas_call(functools.partial(kernel, sizes), out_shape=[pltpu.VMEM((J...]
    pallas_call x1, Pallas kernels: 4.12 us -> 9.25 us  [shards(): pl.pallas_call(functools.partial(finish, sizes), out_shape=[pltpu.VMEM(ou...]
    ppermute x2 -> x1, starting transfers between devices: 3.06 us -> 0.07 us  [cross(): return lax.ppermute(block, 'lat', [(0, 1), (1, 0)])]
    ppermute x2 -> x1, waiting for transfers between devices: 14.5 us -> 17.1 us  [cross(): return lax.ppermute(block, 'lat', [(0, 1), (1, 0)])]
  transfers between devices with their start and end apart: 2 -> 1, of which waited for: 1 -> 1; matrix products, arithmetic and copies ran while one was open for 0% -> 0% of each run, Pallas kernels for 3% -> 3%
where the time goes in v3:
time: 147 us; the launch traced here: 146 us
  Pallas kernels  128 us (87%)
  waiting for transfers between devices  17.1 us (12%)
    pallas_call x1, Pallas kernels, shards(): pl.pallas_call(functools.partial(kernel, sizes), out_shape=[pltpu.VMEM((J...  113 us
    ppermute x1, waiting for transfers between devices, cross(): return lax.ppermute(block, 'lat', [(0, 1), (1, 0)])  17.1 us
    pallas_call x1, Pallas kernels, shards(): pl.pallas_call(functools.partial(finish, sizes), out_shape=[pltpu.VMEM(ou...  9.25 us
    pallas_call x1, Pallas kernels, shards(): pl.pallas_call(functools.partial(write_early, sizes), out_shape=[whole] *...  5.02 us
  transfers between devices with their start and end apart: 1, of which 1 were waited for; matrix products, arithmetic and copies ran while one was open for 0% of the time, Pallas kernels for 3%

profile of v3, /device:TPU:0, one launch (start us, length us, event | category | flops | bytes accessed | tf_op | source)
XLA Modules:
  0.0 146.4 jit_solution(8374398281681133310)
XLA Ops:
  0.6 112.5 %shard_map.50 = (f32[4,128,32,128]{3,2,1,0:T(8,128)S(1)}, f32[4,32,128]{2,1,0:T(8,128)S(1)}, f32[4,32,128]{2,1,0:T(8,128)S(1)}, f32[1,128,32,128]{3,2,1,0:T(8,12...) custom-call(f32[4,128,32,128]{3,2,1,0:T(8,128)} %tracer.1, ...), custom_call_target="tpu_custom_call" | custom-call | tf_op jit(solution)/shard_map/pallas_call | solution.py:492
  113.1 0.1 collective-permute-start
  113.2 5.0 %shard_map.52 = (f32[4,128,32,128]{3,2,1,0:T(8,128)}, f32[4,128,32,128]{3,2,1,0:T(8,128)}) custom-call(f32[4,128,32,128]{3,2,1,0:T(8,128)S(1)} %get-tuple-element.14.end, f32[4,32,128]{2,1,0:T(8,128)S(1)} %get-tuple-element.22.mean, f32[4,32,128]{2,1,0:T(8,128)S(1)} %get-tuple-element.23.scale), custom_call_target="tpu_custom_call" | custom-call | flops 4294967296 | bytes 12582912 | tf_op jit(solution)/shard_map/pallas_call | solution.py:521
  118.3 17.1 %collective-permute-done.halo = f32[1,128,16,128]{3,2,1,0:T(8,128)S(1)} collective-permute-done((f32[1,128,16,128]{3,2,1,0:T(8,128)S(1)}, f32[1,128,16,128]{3,2,1,0:T(8,128)S(1)}, u32[]{:S(2)}, u32[]{:S(2)}) %collective-permute-start) | collective-permute-done | bytes 1048608 | tf_op jit(solution)/shard_map/ppermute | solution.py:468
  135.4 9.3 %shard_map.51 = (f32[1,128,16,128]{3,2,1,0:T(8,128)S(1)}, f32[1,32,128]{2,1,0:T(8,128)S(1)}, f32[1,32,128]{2,1,0:T(8,128)S(1)}) custom-call(f32[1,128,32,128]{3,2,1,0:T(8,128)S(1)} %get-tuple-element.15.base, f32[1,128,16,128]{3,2,1,0:T(8,128)S(1)} %get-tuple-element.16.factor, f32[4,1,2,8,128]{4,3,2,1,0:T(8,128)S(1)} %get-tuple-element.17.sums_in, ...), custom_call_target="tpu_custom_call" | custom-call | tf_op jit(solution)/shard_map/pallas_call | solution.py:531
  144.7 1.7 %shard_map.53 = (f32[4,128,32,128]{3,2,1,0:T(8,128)}, f32[4,128,32,128]{3,2,1,0:T(8,128)}) custom-call(f32[4,128,32,128]{3,2,1,0:T(8,128)S(1)} %get-tuple-element.14.end, f32[1,128,16,128]{3,2,1,0:T(8,128)S(1)} %get-tuple-element.19.tail, f32[1,32,128]{2,1,0:T(8,128)S(1)} %get-tuple-element.20.mean, ...), custom_call_target="tpu_custom_call", output_to_operand_aliasing={{0}: (4, {}), {1}: (5, {})} | custom-call | tf_op jit(solution)/shard_map/pallas_call | solution.py:546
Async XLA Ops:
  113.1 22.3 %collective-permute-start = (f32[1,128,16,128]{3,2,1,0:T(8,128)S(1)}, f32[1,128,16,128]{3,2,1,0:T(8,128)S(1)}, u32[]{:S(2)}, u32[]{:S(2)}) collective-permute-start(f32[1,128,16,128]{3,2,1,0:T(8,128)S(1)} %get-tuple-element.18), channel_id=1, source_target_pairs={{0,16},{16,0},{1,17},{17,1},{2,18},{18,2},{3,19},{19,3},{4,20},{20... | collective-permute-start | bytes 3145736 | tf_op jit(solution)/shard_map/ppermute | solution.py:468

commit v4 on v3

--- a/solution.py
+++ b/solution.py
@@ -357,14 +357,9 @@
             when(side[3], lambda: y_copy(STEPS - 1, chunk, s).wait_send())
 
 
-def finish(
-    sizes, base, factor, sums_in, halo, tail, mean_out, scale_out, sums, peer_sums, send_sem, recv_sem,
-):
-    n_lat, n_lon, _ = sizes
-    late, I, K, M = base.shape
-    chunks, blocks, stay = K // TILE, I // ROWS, kept(K)
+def settle(sizes, sums, mean_out, scale_out, peer_sums, send_sem, recv_sem, count, between):
+    n_lon = sizes[1]
     lon = lax.axis_index("lon")
-
     barrier = pltpu.get_barrier_semaphore()
     for shift in range(1, n_lon):
         pl.semaphore_signal(barrier, inc=1, device_id={"lon": lax.rem(lon + shift, n_lon)},
@@ -376,50 +371,66 @@
             send_sem=send_sem.at[shift - 1], recv_sem=recv_sem.at[shift - 1],
             device_id={"lon": lax.rem(lon + shift, n_lon)}, device_id_type=MESH)
 
-    zero = jnp.zeros((TILE, M), jnp.float32)
-    for s in range(late):
-        for chunk in range(stay):
-            for q in range(2):
-                sums[chunk, s, q] = sums_in[chunk, s, q]
-        for chunk in range(stay, chunks):
-            here, there = pl.ds(chunk * TILE, TILE), pl.ds((chunk - stay) * TILE, TILE)
-
-            def body(b, totals):
-                r = pl.ds(b * ROWS, ROWS)
-                new = base[s, r, here, :] + factor[s, r, there, :] * halo[s, r, there, :]
-                tail[s, r, there, :] = new
-                return tally(new, totals)
-
-            totals = lax.fori_loop(0, blocks, body, (zero, zero))
-            for q in range(2):
-                sums[chunk, s, q] = totals[q]
-
+    between()
     pl.semaphore_wait(barrier, n_lon - 1)
     for shift in range(1, n_lon):
         copy(shift).start()
     for shift in range(1, n_lon):
         copy(shift).wait_recv()
-    for s in range(late):
-        for chunk in range(chunks):
+    for chunk in range(sums.shape[0]):
+        for s in range(sums.shape[1]):
             total = [sums[chunk, s, q] for q in range(2)]
             for shift in range(1, n_lon):
                 total = [total[q] + peer_sums[shift - 1, chunk, s, q] for q in range(2)]
             here = pl.ds(chunk * TILE, TILE)
-            mean_out[s, here, :], scale_out[s, here, :] = close(total, I * n_lon)
+            mean_out[s, here, :], scale_out[s, here, :] = close(total, count)
     for shift in range(1, n_lon):
         copy(shift).wait_send()
 
 
-def write_early(sizes, end, mean, scale, standardized, end_out, held, sem):
+def settle_kept(sizes, count, sums_in, mean_out, scale_out, sums, peer_sums, send_sem, recv_sem):
+    def between():
+        sums[...] = sums_in[...]
+
+    settle(sizes, sums, mean_out, scale_out, peer_sums, send_sem, recv_sem, count, between)
+
+
+def finish(sizes, count, base, factor, halo, tail, mean_out, scale_out, sums, peer_sums, send_sem, recv_sem):
+    late, I, K, M = base.shape
+    high = halo.shape[2]
+
+    def between():
+        zero = jnp.zeros((TILE, M), jnp.float32)
+        for s in range(late):
+            for chunk in range(high // TILE):
+                here, there = pl.ds(K - high + chunk * TILE, TILE), pl.ds(chunk * TILE, TILE)
+
+                def body(b, totals):
+                    r = pl.ds(b * ROWS, ROWS)
+                    new = base[s, r, here, :] + factor[s, r, there, :] * halo[s, r, there, :]
+                    tail[s, r, there, :] = new
+                    return tally(new, totals)
+
+                totals = lax.fori_loop(0, I // ROWS, body, (zero, zero))
+                for q in range(2):
+                    sums[chunk, s, q] = totals[q]
+
+    settle(sizes, sums, mean_out, scale_out, peer_sums, send_sem, recv_sem, count, between)
+
+
+def write_early(
+    sizes, end, mean, scale, mean_kept, scale_kept, standardized, end_out, held, held_kept, sem,
+):
     J, I, K, M = end.shape
     lat = lax.axis_index("lat")
     first, number = early_planes(sizes[0], lat, J)
+    sides = lat_sides(sizes[0], lat, J)
     done = pl.ds(0, kept(K) * TILE)
     copies = [pltpu.make_async_copy(
-        end.at[pl.ds(first, number)], end_out.at[pl.ds(first, number)], sem.at[number])]
-    for s, side in enumerate(lat_sides(sizes[0], lat, J)):
+        end.at[pl.ds(first, number)], end_out.at[pl.ds(first, number)], sem.at[0])]
+    for s, side in enumerate(sides):
         copies.append(pltpu.make_async_copy(
-            end.at[side[0], :, done, :], end_out.at[side[0], :, done, :], sem.at[number + 1 + s]))
+            end.at[side[0], :, done, :], end_out.at[side[0], :, done, :], sem.at[1 + s]))
     for copy in copies:
         copy.start()
     for p in range(number):
@@ -431,32 +442,44 @@
             rows = pl.ds(b * ROWS, ROWS)
             held[p, rows] = (end[j, rows] - offset) * factor
 
-        copies.append(pltpu.make_async_copy(held.at[p], standardized.at[j], sem.at[p]))
+        copies.append(pltpu.make_async_copy(
+            held.at[p], standardized.at[j], sem.at[1 + len(sides) + p]))
+        copies[-1].start()
+    for s, side in enumerate(sides):
+        offset, factor = mean_kept[s], scale_kept[s]
+
+        @pl.loop(0, I // ROWS)
+        def _(b):
+            rows = pl.ds(b * ROWS, ROWS)
+            held_kept[s, rows] = (end[side[0], rows, done, :] - offset) * factor
+
+        copies.append(pltpu.make_async_copy(
+            held_kept.at[s], standardized.at[side[0], :, done, :], sem.at[1 + len(sides) + number + s]))
         copies[-1].start()
     for copy in copies:
         copy.wait()
 
 
-def write_late(sizes, end, tail, mean, scale, old_standardized, old_end, standardized, end_out, held, sem):
-    J, I, K, M = end.shape
-    cut = kept(K) * TILE
-    low, high = pl.ds(0, cut), pl.ds(cut, K - cut)
+def write_late(sizes, tail, mean, scale, old_standardized, old_end, standardized, end_out, held, sem):
+    late, I, high, M = tail.shape
+    J, K = end_out.shape[0], end_out.shape[2]
+    here = pl.ds(K - high, high)
+    half = I // 2
     copies = []
     for s, side in enumerate(lat_sides(sizes[0], lax.axis_index("lat"), J)):
         j = side[0]
-        copies.append(pltpu.make_async_copy(tail.at[s], end_out.at[j, :, high, :], sem.at[s, 0]))
+        copies.append(pltpu.make_async_copy(tail.at[s], end_out.at[j, :, here, :], sem.at[s, 0]))
         copies[-1].start()
-        for n, here in enumerate((low, high)):
-            offset, scaling = mean[s, here, :], scale[s, here, :]
-
-            @pl.loop(0, I // ROWS)
+        offset, scaling = mean[s], scale[s]
+        for n in range(2):
+            @pl.loop(0, half // ROWS)
             def _(b):
-                rows = pl.ds(b * ROWS, ROWS)
-                new = end[j, rows, here, :] if n == 0 else tail[s, rows]
-                held[s, rows, here, :] = (new - offset) * scaling
-
+                rows = pl.ds(n * half + b * ROWS, ROWS)
+                held[s, rows] = (tail[s, rows] - offset) * scaling
+
+            part = pl.ds(n * half, half)
             copies.append(pltpu.make_async_copy(
-                held.at[s, :, here, :], standardized.at[j, :, here, :], sem.at[s, 1 + n]))
+                held.at[s, part], standardized.at[j, part, here, :], sem.at[s, 1 + n]))
             copies[-1].start()
     for copy in copies:
         copy.wait()
@@ -498,7 +521,7 @@
             pltpu.VMEM((late, I, K, M), f32),
             pltpu.VMEM(out_of, f32),
             pltpu.VMEM(out_of, f32),
-            pltpu.VMEM((chunks, late, 2, TILE, M), f32),
+            pltpu.VMEM((stay, late, 2, TILE, M), f32),
         ],
         in_specs=[hbm] * 3,
         out_specs=[vmem] * 7,
@@ -518,40 +541,56 @@
     )(tracer, conductance, source)
     halo = cross(sizes, out)
     whole = jax.ShapeDtypeStruct((J, I, K, M), f32)
+
+    def exchange_of(pieces):
+        return [
+            pltpu.VMEM((pieces, late, 2, TILE, M), f32),
+            pltpu.VMEM((peers, pieces, late, 2, TILE, M), f32),
+            dma((peers,)),
+            dma((peers,)),
+        ]
+
+    mean_kept, scale_kept = pl.pallas_call(
+        functools.partial(settle_kept, sizes, I * n_lon),
+        out_shape=[pltpu.VMEM((late, stay * TILE, M), f32)] * 2,
+        in_specs=[vmem],
+        out_specs=[vmem] * 2,
+        scratch_shapes=exchange_of(stay),
+        compiler_params=pltpu.CompilerParams(
+            collective_id=1, has_side_effects=True, vmem_limit_bytes=4 << 20),
+        cost_estimate=pl.CostEstimate(flops=1 << 31, bytes_accessed=1 << 16, transcendentals=0),
+    )(sums)
     standardized, end_out = pl.pallas_call(
         functools.partial(write_early, sizes),
         out_shape=[whole] * 2,
-        in_specs=[vmem] * 3,
+        in_specs=[vmem] * 5,
         out_specs=[hbm] * 2,
-        scratch_shapes=[pltpu.VMEM((early, I, K, M), f32), dma((early + 1 + late,))],
+        scratch_shapes=[
+            pltpu.VMEM((early, I, K, M), f32), pltpu.VMEM((late, I, stay * TILE, M), f32),
+            dma((1 + early + 2 * late,)),
+        ],
         compiler_params=pltpu.CompilerParams(vmem_limit_bytes=16 << 20),
         cost_estimate=pl.CostEstimate(
             flops=1 << 32, bytes_accessed=8 * early * I * K * M, transcendentals=0),
-    )(end, mean, scale)
+    )(end, mean, scale, mean_kept, scale_kept)
     tail, mean, scale = pl.pallas_call(
-        functools.partial(finish, sizes),
-        out_shape=[
-            pltpu.VMEM(out_of, f32), pltpu.VMEM((late, K, M), f32), pltpu.VMEM((late, K, M), f32)],
-        in_specs=[vmem] * 4,
+        functools.partial(finish, sizes, I * n_lon),
+        out_shape=[pltpu.VMEM(out_of, f32)] + [pltpu.VMEM((late, K - stay * TILE, M), f32)] * 2,
+        in_specs=[vmem] * 3,
         out_specs=[vmem] * 3,
-        scratch_shapes=[
-            pltpu.VMEM((chunks, late, 2, TILE, M), f32),
-            pltpu.VMEM((peers, chunks, late, 2, TILE, M), f32),
-            dma((peers,)),
-            dma((peers,)),
-        ],
+        scratch_shapes=exchange_of(chunks - stay),
         compiler_params=pltpu.CompilerParams(
-            collective_id=1, has_side_effects=True, vmem_limit_bytes=4 << 20),
-    )(base, factor, sums, halo)
+            collective_id=2, has_side_effects=True, vmem_limit_bytes=4 << 20),
+    )(base, factor, halo)
     return pl.pallas_call(
         functools.partial(write_late, sizes),
         out_shape=[whole] * 2,
-        in_specs=[vmem] * 4 + [hbm] * 2,
+        in_specs=[vmem] * 3 + [hbm] * 2,
         out_specs=[hbm] * 2,
-        input_output_aliases={4: 0, 5: 1},
-        scratch_shapes=[pltpu.VMEM((late, I, K, M), f32), dma((late, 3))],
+        input_output_aliases={3: 0, 4: 1},
+        scratch_shapes=[pltpu.VMEM(out_of, f32), dma((late, 3))],
         compiler_params=pltpu.CompilerParams(vmem_limit_bytes=8 << 20),
-    )(end, tail, mean, scale, standardized, end_out)
+    )(tail, mean, scale, standardized, end_out)
 
 
 def solution(mesh):

time: 147 us -> 146 us (level)
  waiting for transfers between devices: 17.1 us -> 4.39 us
  Pallas kernels: 128 us -> 140 us
    ppermute x1, waiting for transfers between devices: 17.1 us -> 4.39 us  [cross(): return lax.ppermute(block, 'lat', [(0, 1), (1, 0)])]
    pallas_call x1 -> x2, Pallas kernels: 9.25 us -> 21.3 us  [the longest x1 12.5 us: shards(): pl.pallas_call(functools.partial(settle_kept, sizes, I * n_lon), out_shap...]
  transfers between devices with their start and end apart: 1 -> 1, of which waited for: 1 -> 1; matrix products, arithmetic and copies ran while one was open for 0% -> 0% of each run, Pallas kernels for 3% -> 12%
where the time goes in v4:
time: 146 us
  Pallas kernels  140 us (96%)
  waiting for transfers between devices  4.39 us (3%)
    pallas_call x1, Pallas kernels, shards(): pl.pallas_call(functools.partial(kernel, sizes), out_shape=[pltpu.VMEM((J...  113 us
    pallas_call x1, Pallas kernels, shards(): pl.pallas_call(functools.partial(settle_kept, sizes, I * n_lon), out_shap...  12.5 us
    pallas_call x1, Pallas kernels, shards(): pl.pallas_call(functools.partial(finish, sizes, I * n_lon), out_shape=[pl...  8.84 us
    pallas_call x1, Pallas kernels, shards(): pl.pallas_call(functools.partial(write_early, sizes), out_shape=[whole] *...  5.31 us
    ppermute x1, waiting for transfers between devices, cross(): return lax.ppermute(block, 'lat', [(0, 1), (1, 0)])  4.39 us
  transfers between devices with their start and end apart: 1, of which 1 were waited for; matrix products, arithmetic and copies ran while one was open for 0% of the time, Pallas kernels for 12%

profile of v4, /device:TPU:0, one launch (start us, length us, event | category | flops | bytes accessed | tf_op | source)
XLA Modules:
  0.0 145.6 jit_solution(2420970331405111496)
XLA Ops:
  0.6 112.5 %shard_map.50 = (f32[4,128,32,128]{3,2,1,0:T(8,128)S(1)}, f32[4,32,128]{2,1,0:T(8,128)S(1)}, f32[4,32,128]{2,1,0:T(8,128)S(1)}, f32[1,128,32,128]{3,2,1,0:T(8,12...) custom-call(f32[4,128,32,128]{3,2,1,0:T(8,128)} %tracer.1, ...), custom_call_target="tpu_custom_call" | custom-call | tf_op jit(solution)/shard_map/pallas_call | solution.py:515
  113.1 0.1 collective-permute-start
  113.2 12.5 %shard_map.52 = (f32[1,16,128]{2,1,0:T(8,128)S(1)}, f32[1,16,128]{2,1,0:T(8,128)S(1)}) custom-call(f32[2,1,2,8,128]{4,3,2,1,0:T(8,128)S(1)} %get-tuple-element.25.sums_in), custom_call_target="tpu_custom_call" | custom-call | flops 2147483648 | bytes 65536 | tf_op jit(solution)/shard_map/pallas_call | solution.py:553
  125.7 5.3 %shard_map.53 = (f32[4,128,32,128]{3,2,1,0:T(8,128)}, f32[4,128,32,128]{3,2,1,0:T(8,128)}) custom-call(f32[4,128,32,128]{3,2,1,0:T(8,128)S(1)} %get-tuple-element.22.end, f32[4,32,128]{2,1,0:T(8,128)S(1)} %get-tuple-element.23.mean, f32[4,32,128]{2,1,0:T(8,128)S(1)} %get-tuple-element.24.scale, f32[1,16,128]{2,1,0:T(8,128)S(1)} %get-tuple-element.26.mean_kept, ...), custom_call_target="tpu_custom_call" | custom-call | flops 4294967296 | bytes 12582912 | tf_op jit(solution)/shard_map/pallas_call | solution.py:563
  131.0 4.4 %collective-permute-done.halo = f32[1,128,16,128]{3,2,1,0:T(8,128)S(1)} collective-permute-done((f32[1,128,16,128]{3,2,1,0:T(8,128)S(1)}, f32[1,128,16,128]{3,2,1,0:T(8,128)S(1)}, u32[]{:S(2)}, u32[]{:S(2)}) %collective-permute-start) | collective-permute-done | bytes 1048608 | tf_op jit(solution)/shard_map/ppermute | solution.py:491
  135.4 8.8 %shard_map.51 = (f32[1,128,16,128]{3,2,1,0:T(8,128)S(1)}, f32[1,16,128]{2,1,0:T(8,128)S(1)}, f32[1,16,128]{2,1,0:T(8,128)S(1)}) custom-call(f32[1,128,32,128]{3,2,1,0:T(8,128)S(1)} %get-tuple-element.16.base, f32[1,128,16,128]{3,2,1,0:T(8,128)S(1)} %get-tuple-element.17.factor, f32[1,128,16,128]{3,2,1,0:T(8,128)S(1)} %collective-permute-done.halo), custom_call_target="tpu_custom_call" | custom-call | tf_op jit(solution)/shard_map/pallas_call | solution.py:576
  144.2 1.4 shard_map.54
Async XLA Ops:
  113.1 22.3 %collective-permute-start = (f32[1,128,16,128]{3,2,1,0:T(8,128)S(1)}, f32[1,128,16,128]{3,2,1,0:T(8,128)S(1)}, u32[]{:S(2)}, u32[]{:S(2)}) collective-permute-start(f32[1,128,16,128]{3,2,1,0:T(8,128)S(1)} %get-tuple-element.18), channel_id=1, source_target_pairs={{0,16},{16,0},{1,17},{17,1},{2,18},{18,2},{3,19},{19,3},{4,20},{20... | collective-permute-start | bytes 3145736 | tf_op jit(solution)/shard_map/ppermute | solution.py:491

commit v5 on v4

--- a/solution.py
+++ b/solution.py
@@ -52,7 +52,8 @@
 def kernel(
     sizes, tracer, conductance, source, end, mean_out, scale_out, base, factor, out, sums_late,
     even, odd, cond, sour, y_halo, z_lower, z_upper, z_first, z_last, sums_early, peer_early,
-    load_sem, y_send, y_recv, x_send, x_recv, z_send, z_recv, early_send, early_recv,
+    peer_in, all_in,
+    load_sem, first_sem, y_send, y_recv, x_send, x_recv, z_send, z_recv, early_send, early_recv,
 ):
     n_lat, n_lon, n_lev = sizes
     J, I, K, M = tracer.shape
@@ -122,39 +123,51 @@
     def arrives(axis, way, act):
         pl.when((below if way == 0 else above)[axis])(act)
 
+    first_loads = [[
+        pltpu.make_async_copy(
+            tracer.at[side[0], :, levels(chunk), :], even.at[side[0], rows_in, levels(chunk), :],
+            first_sem.at[chunk, s])
+        for s, side in enumerate(sides)] for chunk in range(chunks)]
+    loads = [
+        pltpu.make_async_copy(
+            tracer.at[pl.ds(first, number)], even.at[pl.ds(first, number), rows_in], load_sem.at[0]),
+        pltpu.make_async_copy(conductance, cond, load_sem.at[1]),
+        pltpu.make_async_copy(source, sour, load_sem.at[2]),
+    ]
+    for chunk in range(chunks):
+        for load in first_loads[chunk]:
+            load.start()
+    even_lat = lat % 2 == 0
+    around = n_lon - 1 + below["lev"].astype(jnp.int32) + above["lev"].astype(jnp.int32)
+    met = jnp.where(even_lat, around, 0)
     barrier = pltpu.get_barrier_semaphore()
-    met = n_lon - 1
+
+    def signal_around(semaphore):
+        for shift in range(1, n_lon):
+            pl.semaphore_signal(semaphore, inc=1, device_id={"lon": lax.rem(lon + shift, n_lon)},
+                                device_id_type=MESH)
+        for way in (0, 1):
+            sends("lev", way, lambda: pl.semaphore_signal(
+                semaphore, inc=1, device_id=target("lev", way), device_id_type=MESH))
+
     for _, _, peer, exists, _ in sides:
         when(exists, lambda: pl.semaphore_signal(
             barrier, inc=1, device_id={"lat": peer}, device_id_type=MESH))
         met = met + (1 if exists is None else exists.astype(jnp.int32))
-    for way in (0, 1):
-        sends("lev", way, lambda: pl.semaphore_signal(
-            barrier, inc=1, device_id=target("lev", way), device_id_type=MESH))
-        met = met + (above if way == 0 else below)["lev"].astype(jnp.int32)
-    for shift in range(1, n_lon):
-        pl.semaphore_signal(barrier, inc=1, device_id={"lon": lax.rem(lon + shift, n_lon)},
-                            device_id_type=MESH)
-
-    loads = [
-        pltpu.make_async_copy(tracer.at[plane], even.at[plane, rows_in], load_sem.at[3 + s])
-        for s, (plane, _, _, _, _) in enumerate(sides)
-    ]
-    loads.append(pltpu.make_async_copy(
-        tracer.at[pl.ds(first, number)], even.at[pl.ds(first, number), rows_in], load_sem.at[0]))
-    loads.append(pltpu.make_async_copy(conductance, cond, load_sem.at[1]))
-    loads.append(pltpu.make_async_copy(source, sour, load_sem.at[2]))
-    for load in loads[:-2]:
-        load.start()
-    for load in loads[:-3]:
-        load.wait()
+    pl.when(even_lat)(lambda: signal_around(barrier))
+    loads[0].start()
     pl.semaphore_wait(barrier, met)
 
     for chunk in range(chunks):
         for s, side in enumerate(sides):
+            first_loads[chunk][s].wait()
             when(side[3], lambda: y_copy(0, chunk, s).start())
-    loads[-2].start()
-    loads[-1].start()
+    loads[1].start()
+    loads[2].start()
+
+    @pl.when(even_lat)
+    def _():
+        signal_around(peer_in)
 
     for s, side in enumerate(sides):
         if side[3] is not None:
@@ -293,11 +306,21 @@
             condition = jnp.logical_and(condition, exists)
         when(exists if condition is None else condition, lambda: y_copy(step, chunk, s).start())
 
-    loads[-3].wait()
+    @pl.when(even_lat)
+    def _():
+        pl.semaphore_wait(peer_in, around)
+        pl.when(lat < n_lat - 1)(lambda: pl.semaphore_signal(
+            all_in, inc=1, device_id={"lat": lat + 1}, device_id_type=MESH))
+
+    @pl.when(jnp.logical_not(even_lat))
+    def _():
+        pl.semaphore_wait(all_in, 1)
+
+    loads[0].wait()
     for part in range(len(faces)):
         pack_and_send(0, part)
-    loads[-2].wait()
-    loads[-1].wait()
+    loads[1].wait()
+    loads[2].wait()
     for step in range(STEPS):
         last = step == STEPS - 1
         if step >= 1:
@@ -526,7 +549,10 @@
         in_specs=[hbm] * 3,
         out_specs=[vmem] * 7,
         scratch_shapes=[pltpu.VMEM(shape, f32) for shape in scratch] + [
-            dma((3 + late,)),
+            pltpu.SemaphoreType.REGULAR,
+            pltpu.SemaphoreType.REGULAR,
+            dma((3,)),
+            dma((chunks, late)),
             dma((STEPS, chunks, late)),
             dma((STEPS, chunks, late)),
             dma((STEPS, 2, 1 + late)),

time: 146 us -> 145 us (level)
  starting transfers between devices: 0.07 us -> 2.08 us
  Pallas kernels: 140 us -> 138 us
    ppermute x1, starting transfers between devices: 0.07 us -> 2.08 us  [cross(): return lax.ppermute(block, 'lat', [(0, 1), (1, 0)])]
  transfers between devices with their start and end apart: 1 -> 1, of which waited for: 1 -> 1; matrix products, arithmetic and copies ran while one was open for 0% -> 0% of each run, Pallas kernels for 12% -> 11%
where the time goes in v5:
time: 145 us
  Pallas kernels  138 us (95%)
  waiting for transfers between devices  3.77 us (3%)
  starting transfers between devices  2.08 us (1%)
    pallas_call x1, Pallas kernels, shards(): pl.pallas_call(functools.partial(kernel, sizes), out_shape=[pltpu.VMEM((J...  111 us
    pallas_call x1, Pallas kernels, shards(): pl.pallas_call(functools.partial(settle_kept, sizes, I * n_lon), out_shap...  11 us
    pallas_call x1, Pallas kernels, shards(): pl.pallas_call(functools.partial(finish, sizes, I * n_lon), out_shape=[pl...  9.43 us
    pallas_call x1, Pallas kernels, shards(): pl.pallas_call(functools.partial(write_early, sizes), out_shape=[whole] *...  5.31 us
    ppermute x1, waiting for transfers between devices, cross(): return lax.ppermute(block, 'lat', [(0, 1), (1, 0)])  3.77 us
  transfers between devices with their start and end apart: 1, of which 1 were waited for; matrix products, arithmetic and copies ran while one was open for 0% of the time, Pallas kernels for 11%

profile of v5, /device:TPU:0, one launch (start us, length us, event | category | flops | bytes accessed | tf_op | source)
XLA Modules:
  0.0 144.9 jit_solution(14767519282803855401)
XLA Ops:
  0.6 111.2 %shard_map.50 = (f32[4,128,32,128]{3,2,1,0:T(8,128)S(1)}, f32[4,32,128]{2,1,0:T(8,128)S(1)}, f32[4,32,128]{2,1,0:T(8,128)S(1)}, f32[1,128,32,128]{3,2,1,0:T(8,12...) custom-call(f32[4,128,32,128]{3,2,1,0:T(8,128)} %tracer.1, ...), custom_call_target="tpu_custom_call" | custom-call | tf_op jit(solution)/shard_map/pallas_call | solution.py:538
  111.9 2.1 %collective-permute-start = (f32[1,128,16,128]{3,2,1,0:T(8,128)S(1)}, f32[1,128,16,128]{3,2,1,0:T(8,128)S(1)}, u32[]{:S(2)}, u32[]{:S(2)}) collective-permute-start(f32[1,128,16,128]{3,2,1,0:T(8,128)S(1)} %get-tuple-element.18), channel_id=1, source_target_pairs={{0,16},{16,0},{1,17},{17,1},{2,18},{18,2},{3,19},{19,3},{4,20},{20... | collective-permute-start | bytes 3145736 | tf_op jit(solution)/shard_map/ppermute | solution.py:514
  114.0 11.0 %shard_map.52 = (f32[1,16,128]{2,1,0:T(8,128)S(1)}, f32[1,16,128]{2,1,0:T(8,128)S(1)}) custom-call(f32[2,1,2,8,128]{4,3,2,1,0:T(8,128)S(1)} %get-tuple-element.25.sums_in), custom_call_target="tpu_custom_call" | custom-call | flops 2147483648 | bytes 65536 | tf_op jit(solution)/shard_map/pallas_call | solution.py:579
  125.0 5.3 %shard_map.53 = (f32[4,128,32,128]{3,2,1,0:T(8,128)}, f32[4,128,32,128]{3,2,1,0:T(8,128)}) custom-call(f32[4,128,32,128]{3,2,1,0:T(8,128)S(1)} %get-tuple-element.22.end, f32[4,32,128]{2,1,0:T(8,128)S(1)} %get-tuple-element.23.mean, f32[4,32,128]{2,1,0:T(8,128)S(1)} %get-tuple-element.24.scale, f32[1,16,128]{2,1,0:T(8,128)S(1)} %get-tuple-element.26.mean_kept, ...), custom_call_target="tpu_custom_call" | custom-call | flops 4294967296 | bytes 12582912 | tf_op jit(solution)/shard_map/pallas_call | solution.py:589
  130.3 3.8 %collective-permute-done.halo = f32[1,128,16,128]{3,2,1,0:T(8,128)S(1)} collective-permute-done((f32[1,128,16,128]{3,2,1,0:T(8,128)S(1)}, f32[1,128,16,128]{3,2,1,0:T(8,128)S(1)}, u32[]{:S(2)}, u32[]{:S(2)}) %collective-permute-start) | collective-permute-done | bytes 1048608 | tf_op jit(solution)/shard_map/ppermute | solution.py:514
  134.1 9.4 %shard_map.51 = (f32[1,128,16,128]{3,2,1,0:T(8,128)S(1)}, f32[1,16,128]{2,1,0:T(8,128)S(1)}, f32[1,16,128]{2,1,0:T(8,128)S(1)}) custom-call(f32[1,128,32,128]{3,2,1,0:T(8,128)S(1)} %get-tuple-element.16.base, f32[1,128,16,128]{3,2,1,0:T(8,128)S(1)} %get-tuple-element.17.factor, f32[1,128,16,128]{3,2,1,0:T(8,128)S(1)} %collective-permute-done.halo), custom_call_target="tpu_custom_call" | custom-call | tf_op jit(solution)/shard_map/pallas_call | solution.py:602
  143.5 1.4 shard_map.54
Async XLA Ops:
  111.9 22.2 %collective-permute-start = (f32[1,128,16,128]{3,2,1,0:T(8,128)S(1)}, f32[1,128,16,128]{3,2,1,0:T(8,128)S(1)}, u32[]{:S(2)}, u32[]{:S(2)}) collective-permute-start(f32[1,128,16,128]{3,2,1,0:T(8,128)S(1)} %get-tuple-element.18), channel_id=1, source_target_pairs={{0,16},{16,0},{1,17},{17,1},{2,18},{18,2},{3,19},{19,3},{4,20},{20... | collective-permute-start | bytes 3145736 | tf_op jit(solution)/shard_map/ppermute | solution.py:514

commit v6 on v5

--- a/solution.py
+++ b/solution.py
@@ -31,6 +31,11 @@
     return K // TILE // 2
 
 
+def spans(K):
+    start, last = kept(K) * TILE, K - TILE
+    return [(low, high) for low, high in ((start, last), (last, K)) if high > low]
+
+
 def close(total, count):
     offset = total[0] / count
     variance = total[1] / count - offset * offset
@@ -49,12 +54,14 @@
         pl.when(condition)(act)
 
 
-def kernel(
-    sizes, tracer, conductance, source, end, mean_out, scale_out, base, factor, out, sums_late,
-    even, odd, cond, sour, y_halo, z_lower, z_upper, z_first, z_last, sums_early, peer_early,
-    peer_in, all_in,
-    load_sem, first_sem, y_send, y_recv, x_send, x_recv, z_send, z_recv, early_send, early_recv,
-):
+def kernel(sizes, tracer, conductance, source, end, mean_out, scale_out, base, factor, sums_late, *rest):
+    cuts = spans(tracer.shape[2])
+    outs = rest[:len(cuts)]
+    (
+        even, odd, cond, sour, y_halo, z_lower, z_upper, z_first, z_last, sums_early, peer_early,
+        peer_in, all_in,
+        load_sem, first_sem, y_send, y_recv, x_send, x_recv, z_send, z_recv, early_send, early_recv,
+    ) = rest[len(cuts):]
     n_lat, n_lon, n_lev = sizes
     J, I, K, M = tracer.shape
     chunks = K // TILE
@@ -268,6 +275,10 @@
         def _(j):
             early_plane(step, chunk, j, None)
 
+        if step == STEPS - 1 and chunk == max(chunks - 2, 0):
+            for held in range(stay):
+                for s in range(len(sides)):
+                    y_start(step, held, s, odd_lon)
         if n_lat == 2:
             early_plane(step, chunk, jnp.where(lat == 0, 0, J - 1), jnp.where(lat == 0, 1, J - 2))
 
@@ -287,8 +298,10 @@
             new = base[s, r, here, :] + cond[plane, r, here, :] * y_halo[step % 2, s, r, here, :]
             if step < STEPS - 1:
                 field[(step + 1) % 2][plane, pl.ds(1 + b * ROWS, ROWS), here, :] = new
-                if step == STEPS - 2 and chunk >= stay:
-                    out[s, r, levels(chunk - stay), :] = new
+                if step == STEPS - 2:
+                    for out, (low, high) in zip(outs, cuts):
+                        if low <= chunk * TILE < high:
+                            out[s, r, pl.ds(chunk * TILE - low, TILE), :] = new
                 return totals
             end[plane, r, here, :] = new
             return tally(new, totals)
@@ -328,10 +341,6 @@
         faces_arrive(step, 0)
         for chunk in range(chunks):
             early_part(step, chunk)
-            if last and chunk == max(chunks - 2, 0):
-                for held in range(stay):
-                    for s in range(len(sides)):
-                        y_start(step, held, s, odd_lon)
         if last:
             for shift in range(1, n_lon):
                 early_copy(shift).start()
@@ -380,80 +389,140 @@
             when(side[3], lambda: y_copy(STEPS - 1, chunk, s).wait_send())
 
 
-def settle(sizes, sums, mean_out, scale_out, peer_sums, send_sem, recv_sem, count, between):
-    n_lon = sizes[1]
-    lon = lax.axis_index("lon")
+def finish(sizes, base, factor, sums_in, end, out, *rest):
+    halos, (
+        tail, ready, mean_out, scale_out, landing, sums, peer_sums, late_in, y_send, y_recv, send_sem, recv_sem,
+    ) = rest[:-12], rest[-12:]
+    n_lat, n_lon, _ = sizes
+    late, I, K, M = base.shape
+    chunks, stay, cuts = K // TILE, kept(K), spans(K)
+    lat, lon = lax.axis_index("lat"), lax.axis_index("lon")
+    even_lon = lon % 2 == 0
+    n_odd = n_lon // 2
+    sides = lat_sides(n_lat, lat, end.shape[0])
+    peers = [lax.rem(lon + shift, n_lon) for shift in range(1, n_lon)]
+    groups = [group for group in (list(range(stay)), list(range(stay, chunks - 1)), [chunks - 1]) if group]
+    pieces = [pl.ds(group[0], len(group)) for group in groups]
+
+    def y_copy(s, slot):
+        return pltpu.make_async_remote_copy(
+            src_ref=out.at[s], dst_ref=landing.at[slot], send_sem=y_send.at[s], recv_sem=y_recv.at[slot],
+            device_id={"lat": sides[s][2]}, device_id_type=MESH)
+
+    def sum_copy(piece, p):
+        return pltpu.make_async_remote_copy(
+            src_ref=sums.at[pieces[piece]], dst_ref=peer_sums.at[p, pieces[piece]],
+            send_sem=send_sem.at[piece, p], recv_sem=recv_sem.at[piece, p],
+            device_id={"lon": peers[p]}, device_id_type=MESH)
+
+    def send_sums(piece):
+        for p in range(n_lon - 1):
+            sum_copy(piece, p).start()
+
+    def add(chunk, s, arrived, start):
+        here = pl.ds(chunk * TILE, TILE)
+        there, came = pl.ds((chunk - stay) * TILE, TILE), pl.ds(chunk * TILE - start, TILE)
+        zero = jnp.zeros((TILE, M), jnp.float32)
+
+        def body(b, totals):
+            r = pl.ds(b * ROWS, ROWS)
+            new = base[s, r, here, :] + factor[s, r, there, :] * arrived[s, r, came, :]
+            tail[s, r, there, :] = new
+            return tally(new, totals)
+
+        totals = lax.fori_loop(0, I // ROWS, body, (zero, zero))
+        for q in range(2):
+            sums[chunk, s, q] = totals[q]
+
     barrier = pltpu.get_barrier_semaphore()
-    for shift in range(1, n_lon):
-        pl.semaphore_signal(barrier, inc=1, device_id={"lon": lax.rem(lon + shift, n_lon)},
-                            device_id_type=MESH)
-
-    def copy(shift):
-        return pltpu.make_async_remote_copy(
-            src_ref=sums, dst_ref=peer_sums.at[shift - 1],
-            send_sem=send_sem.at[shift - 1], recv_sem=recv_sem.at[shift - 1],
-            device_id={"lon": lax.rem(lon + shift, n_lon)}, device_id_type=MESH)
-
-    between()
-    pl.semaphore_wait(barrier, n_lon - 1)
-    for shift in range(1, n_lon):
-        copy(shift).start()
-    for shift in range(1, n_lon):
-        copy(shift).wait_recv()
-    for chunk in range(sums.shape[0]):
-        for s in range(sums.shape[1]):
-            total = [sums[chunk, s, q] for q in range(2)]
-            for shift in range(1, n_lon):
-                total = [total[q] + peer_sums[shift - 1, chunk, s, q] for q in range(2)]
+    met = jnp.where(even_lon, n_lon - n_odd - 1, n_lon - 1)
+    for _, _, peer, exists, _ in sides:
+        when(exists, lambda: pl.semaphore_signal(
+            barrier, inc=1, device_id={"lat": peer}, device_id_type=MESH))
+        met = met + (1 if exists is None else exists.astype(jnp.int32))
+    for peer in peers:
+        pl.when(jnp.logical_or(even_lon, peer % 2 == 1))(lambda: pl.semaphore_signal(
+            barrier, inc=1, device_id={"lon": peer}, device_id_type=MESH))
+    pl.semaphore_wait(barrier, met)
+    for s, side in enumerate(sides):
+        when(side[3], lambda: y_copy(s, side[4]).start())
+
+    @pl.when(jnp.logical_not(even_lon))
+    def _():
+        for peer in peers:
+            pl.when(peer % 2 == 0)(lambda: pl.semaphore_signal(
+                late_in, inc=1, device_id={"lon": peer}, device_id_type=MESH))
+
+    for s, side in enumerate(sides):
+        if side[3] is not None:
+            @pl.when(jnp.logical_not(side[3]))
+            def _():
+                @pl.loop(0, I // ROWS)
+                def _(b):
+                    landing[s, pl.ds(b * ROWS, ROWS)] = jnp.zeros((ROWS,) + landing.shape[2:], jnp.float32)
+        for chunk in range(chunks - 1):
+            if chunk < stay:
+                for q in range(2):
+                    sums[chunk, s, q] = sums_in[chunk, s, q]
+            else:
+                add(chunk, s, halos[0], cuts[0][0])
+    pl.when(even_lon)(lambda: pl.semaphore_wait(late_in, n_odd))
+    values = {}
+
+    def settle(piece):
+        for p in range(n_lon - 1):
+            sum_copy(piece, p).wait_recv()
+        for chunk in groups[piece]:
+            of_sides = []
+            for s in range(late):
+                total = [sums[chunk, s, q] for q in range(2)]
+                for p in range(n_lon - 1):
+                    total = [total[q] + peer_sums[p, chunk, s, q] for q in range(2)]
+                of_sides.append(close(total, I * n_lon))
+            values[chunk] = [jnp.stack(part) for part in zip(*of_sides)]
+
+    for piece in range(len(groups) - 1):
+        send_sums(piece)
+    for piece, group in enumerate(groups[:-1]):
+        settle(piece)
+        for chunk in group:
             here = pl.ds(chunk * TILE, TILE)
-            mean_out[s, here, :], scale_out[s, here, :] = close(total, count)
-    for shift in range(1, n_lon):
-        copy(shift).wait_send()
-
-
-def settle_kept(sizes, count, sums_in, mean_out, scale_out, sums, peer_sums, send_sem, recv_sem):
-    def between():
-        sums[...] = sums_in[...]
-
-    settle(sizes, sums, mean_out, scale_out, peer_sums, send_sem, recv_sem, count, between)
-
-
-def finish(sizes, count, base, factor, halo, tail, mean_out, scale_out, sums, peer_sums, send_sem, recv_sem):
-    late, I, K, M = base.shape
-    high = halo.shape[2]
-
-    def between():
-        zero = jnp.zeros((TILE, M), jnp.float32)
-        for s in range(late):
-            for chunk in range(high // TILE):
-                here, there = pl.ds(K - high + chunk * TILE, TILE), pl.ds(chunk * TILE, TILE)
-
-                def body(b, totals):
+            for s, side in enumerate(sides):
+                offset, scaling = values[chunk][0][s], values[chunk][1][s]
+
+                @pl.loop(0, I // ROWS)
+                def _(b):
                     r = pl.ds(b * ROWS, ROWS)
-                    new = base[s, r, here, :] + factor[s, r, there, :] * halo[s, r, there, :]
-                    tail[s, r, there, :] = new
-                    return tally(new, totals)
-
-                totals = lax.fori_loop(0, I // ROWS, body, (zero, zero))
-                for q in range(2):
-                    sums[chunk, s, q] = totals[q]
-
-    settle(sizes, sums, mean_out, scale_out, peer_sums, send_sem, recv_sem, count, between)
-
-
-def write_early(
-    sizes, end, mean, scale, mean_kept, scale_kept, standardized, end_out, held, held_kept, sem,
-):
+                    if chunk < stay:
+                        new = end[side[0], r, here, :]
+                    else:
+                        new = tail[s, r, pl.ds((chunk - stay) * TILE, TILE), :]
+                    ready[s, r, here, :] = (new - offset) * scaling
+        for p in range(n_lon - 1):
+            sum_copy(piece, p).wait_send()
+    for s, side in enumerate(sides):
+        when(side[3], lambda: y_copy(s, s).wait_recv())
+        add(chunks - 1, s, landing, (chunks - 1) * TILE)
+    send_sums(len(groups) - 1)
+    for s, side in enumerate(sides):
+        when(side[3], lambda: y_copy(s, side[4]).wait_send())
+
+    settle(len(groups) - 1)
+    mean_out[...], scale_out[...] = values[chunks - 1]
+    for p in range(n_lon - 1):
+        sum_copy(len(groups) - 1, p).wait_send()
+
+
+def write_early(sizes, end, mean, scale, standardized, end_out, held, sem):
     J, I, K, M = end.shape
     lat = lax.axis_index("lat")
     first, number = early_planes(sizes[0], lat, J)
-    sides = lat_sides(sizes[0], lat, J)
     done = pl.ds(0, kept(K) * TILE)
     copies = [pltpu.make_async_copy(
-        end.at[pl.ds(first, number)], end_out.at[pl.ds(first, number)], sem.at[0])]
-    for s, side in enumerate(sides):
+        end.at[pl.ds(first, number)], end_out.at[pl.ds(first, number)], sem.at[number])]
+    for s, side in enumerate(lat_sides(sizes[0], lat, J)):
         copies.append(pltpu.make_async_copy(
-            end.at[side[0], :, done, :], end_out.at[side[0], :, done, :], sem.at[1 + s]))
+            end.at[side[0], :, done, :], end_out.at[side[0], :, done, :], sem.at[number + 1 + s]))
     for copy in copies:
         copy.start()
     for p in range(number):
@@ -465,45 +534,35 @@
             rows = pl.ds(b * ROWS, ROWS)
             held[p, rows] = (end[j, rows] - offset) * factor
 
-        copies.append(pltpu.make_async_copy(
-            held.at[p], standardized.at[j], sem.at[1 + len(sides) + p]))
+        copies.append(pltpu.make_async_copy(held.at[p], standardized.at[j], sem.at[p]))
         copies[-1].start()
-    for s, side in enumerate(sides):
-        offset, factor = mean_kept[s], scale_kept[s]
+    for copy in copies:
+        copy.wait()
+
+
+def write_late(
+    sizes, ready, tail, mean, scale, old_standardized, old_end, standardized, end_out, held, sem,
+):
+    J, K = end_out.shape[0], end_out.shape[2]
+    late, I, high, M = tail.shape
+    copies = []
+    for s, side in enumerate(lat_sides(sizes[0], lax.axis_index("lat"), J)):
+        j = side[0]
+
+        def copy(source, target, rows, n):
+            copies.append(pltpu.make_async_copy(source, target.at[j, :, rows, :], sem.at[s, n]))
+            copies[-1].start()
+
+        copy(ready.at[s], standardized, pl.ds(0, K - TILE), 0)
+        copy(tail.at[s], end_out, pl.ds(K - high, high), 1)
+        offset, scaling = mean[s], scale[s]
 
         @pl.loop(0, I // ROWS)
         def _(b):
             rows = pl.ds(b * ROWS, ROWS)
-            held_kept[s, rows] = (end[side[0], rows, done, :] - offset) * factor
-
-        copies.append(pltpu.make_async_copy(
-            held_kept.at[s], standardized.at[side[0], :, done, :], sem.at[1 + len(sides) + number + s]))
-        copies[-1].start()
-    for copy in copies:
-        copy.wait()
-
-
-def write_late(sizes, tail, mean, scale, old_standardized, old_end, standardized, end_out, held, sem):
-    late, I, high, M = tail.shape
-    J, K = end_out.shape[0], end_out.shape[2]
-    here = pl.ds(K - high, high)
-    half = I // 2
-    copies = []
-    for s, side in enumerate(lat_sides(sizes[0], lax.axis_index("lat"), J)):
-        j = side[0]
-        copies.append(pltpu.make_async_copy(tail.at[s], end_out.at[j, :, here, :], sem.at[s, 0]))
-        copies[-1].start()
-        offset, scaling = mean[s], scale[s]
-        for n in range(2):
-            @pl.loop(0, half // ROWS)
-            def _(b):
-                rows = pl.ds(n * half + b * ROWS, ROWS)
-                held[s, rows] = (tail[s, rows] - offset) * scaling
-
-            part = pl.ds(n * half, half)
-            copies.append(pltpu.make_async_copy(
-                held.at[s, part], standardized.at[j, part, here, :], sem.at[s, 1 + n]))
-            copies[-1].start()
+            held[s, rows] = (tail[s, rows, pl.ds(high - TILE, TILE), :] - offset) * scaling
+
+        copy(held.at[s], standardized, pl.ds(K - TILE, TILE), 2)
     for copy in copies:
         copy.wait()
 
@@ -528,26 +587,25 @@
     early = early_planes(n_lat, 0, J)[1]
     stay = kept(K)
     hbm, vmem = pl.BlockSpec(memory_space=pltpu.HBM), pl.BlockSpec(memory_space=pltpu.VMEM)
-    out_of = (late, I, K - stay * TILE, M)
+    cuts = spans(K)
     scratch = [
         (J, I + 2, K, M), (J, I + 2, K, M), (J, I, K, M), (J, I, K, M), (2, late, I, K, M),
         (2, J, I, 1, M), (2, J, I, 1, M), (2, J, I, 1, M), (2, J, I, 1, M),
         (early, 2, K, M), (peers, early, 2, K, M),
     ]
     limit = sum(4 * math.prod(shape) for shape in scratch) + (2 << 20)
-    end, mean, scale, base, factor, out, sums = pl.pallas_call(
+    end, mean, scale, base, factor, sums, *outs = pl.pallas_call(
         functools.partial(kernel, sizes),
         out_shape=[
             pltpu.VMEM((J, I, K, M), f32),
             pltpu.VMEM((J, K, M), f32),
             pltpu.VMEM((J, K, M), f32),
             pltpu.VMEM((late, I, K, M), f32),
-            pltpu.VMEM(out_of, f32),
-            pltpu.VMEM(out_of, f32),
+            pltpu.VMEM((late, I, K - stay * TILE, M), f32),
             pltpu.VMEM((stay, late, 2, TILE, M), f32),
-        ],
+        ] + [pltpu.VMEM((late, I, high - low, M), f32) for low, high in cuts],
         in_specs=[hbm] * 3,
-        out_specs=[vmem] * 7,
+        out_specs=[vmem] * (6 + len(cuts)),
         scratch_shapes=[pltpu.VMEM(shape, f32) for shape in scratch] + [
             pltpu.SemaphoreType.REGULAR,
             pltpu.SemaphoreType.REGULAR,
@@ -565,58 +623,48 @@
         compiler_params=pltpu.CompilerParams(
             collective_id=0, has_side_effects=True, vmem_limit_bytes=limit),
     )(tracer, conductance, source)
-    halo = cross(sizes, out)
+    halos = [cross(sizes, out) for out in outs[:-1]]
     whole = jax.ShapeDtypeStruct((J, I, K, M), f32)
 
-    def exchange_of(pieces):
-        return [
-            pltpu.VMEM((pieces, late, 2, TILE, M), f32),
-            pltpu.VMEM((peers, pieces, late, 2, TILE, M), f32),
-            dma((peers,)),
-            dma((peers,)),
-        ]
-
-    mean_kept, scale_kept = pl.pallas_call(
-        functools.partial(settle_kept, sizes, I * n_lon),
-        out_shape=[pltpu.VMEM((late, stay * TILE, M), f32)] * 2,
-        in_specs=[vmem],
-        out_specs=[vmem] * 2,
-        scratch_shapes=exchange_of(stay),
-        compiler_params=pltpu.CompilerParams(
-            collective_id=1, has_side_effects=True, vmem_limit_bytes=4 << 20),
-        cost_estimate=pl.CostEstimate(flops=1 << 31, bytes_accessed=1 << 16, transcendentals=0),
-    )(sums)
     standardized, end_out = pl.pallas_call(
         functools.partial(write_early, sizes),
         out_shape=[whole] * 2,
-        in_specs=[vmem] * 5,
+        in_specs=[vmem] * 3,
         out_specs=[hbm] * 2,
-        scratch_shapes=[
-            pltpu.VMEM((early, I, K, M), f32), pltpu.VMEM((late, I, stay * TILE, M), f32),
-            dma((1 + early + 2 * late,)),
-        ],
+        scratch_shapes=[pltpu.VMEM((early, I, K, M), f32), dma((early + 1 + late,))],
         compiler_params=pltpu.CompilerParams(vmem_limit_bytes=16 << 20),
         cost_estimate=pl.CostEstimate(
             flops=1 << 32, bytes_accessed=8 * early * I * K * M, transcendentals=0),
-    )(end, mean, scale, mean_kept, scale_kept)
-    tail, mean, scale = pl.pallas_call(
-        functools.partial(finish, sizes, I * n_lon),
-        out_shape=[pltpu.VMEM(out_of, f32)] + [pltpu.VMEM((late, K - stay * TILE, M), f32)] * 2,
-        in_specs=[vmem] * 3,
-        out_specs=[vmem] * 3,
-        scratch_shapes=exchange_of(chunks - stay),
+    )(end, mean, scale)
+    out_of = (late, I, K - stay * TILE, M)
+    tail, ready, mean, scale = pl.pallas_call(
+        functools.partial(finish, sizes),
+        out_shape=[pltpu.VMEM(out_of, f32), pltpu.VMEM((late, I, K - TILE, M), f32)]
+        + [pltpu.VMEM((late, TILE, M), f32)] * 2,
+        in_specs=[vmem] * (5 + len(halos)),
+        out_specs=[vmem] * 4,
+        scratch_shapes=[
+            pltpu.VMEM((late, I, TILE, M), f32),
+            pltpu.VMEM((chunks, late, 2, TILE, M), f32),
+            pltpu.VMEM((peers, chunks, late, 2, TILE, M), f32),
+            pltpu.SemaphoreType.REGULAR,
+            dma((late,)),
+            dma((late,)),
+            dma((3, peers)),
+            dma((3, peers)),
+        ],
         compiler_params=pltpu.CompilerParams(
-            collective_id=2, has_side_effects=True, vmem_limit_bytes=4 << 20),
-    )(base, factor, halo)
+            collective_id=1, has_side_effects=True, vmem_limit_bytes=8 << 20),
+    )(base, factor, sums, end, outs[-1], *halos)
     return pl.pallas_call(
         functools.partial(write_late, sizes),
         out_shape=[whole] * 2,
-        in_specs=[vmem] * 3 + [hbm] * 2,
+        in_specs=[vmem] * 4 + [hbm] * 2,
         out_specs=[hbm] * 2,
-        input_output_aliases={3: 0, 4: 1},
-        scratch_shapes=[pltpu.VMEM(out_of, f32), dma((late, 3))],
-        compiler_params=pltpu.CompilerParams(vmem_limit_bytes=8 << 20),
-    )(tail, mean, scale, standardized, end_out)
+        input_output_aliases={4: 0, 5: 1},
+        scratch_shapes=[pltpu.VMEM((late, I, TILE, M), f32), dma((late, 3))],
+        compiler_params=pltpu.CompilerParams(vmem_limit_bytes=12 << 20),
+    )(ready, tail, mean, scale, standardized, end_out)
 
 
 def solution(mesh):

time: 145 us -> 145 us (level)
    pallas_call x2 -> x1, Pallas kernels: 20.5 us -> 19.5 us  [shards(): pl.pallas_call(functools.partial(finish, sizes), out_shape=[pltpu.VMEM(ou...]
  transfers between devices with their start and end apart: 1 -> 1, of which waited for: 1 -> 1; matrix products, arithmetic and copies ran while one was open for 0% -> 0% of each run, Pallas kernels for 11% -> 3%
where the time goes in v6:
time: 145 us
  Pallas kernels  138 us (95%)
  waiting for transfers between devices  3.94 us (3%)
  starting transfers between devices  2.07 us (1%)
    pallas_call x1, Pallas kernels, shards(): pl.pallas_call(functools.partial(kernel, sizes), out_shape=[pltpu.VMEM((J...  112 us
    pallas_call x1, Pallas kernels, shards(): pl.pallas_call(functools.partial(finish, sizes), out_shape=[pltpu.VMEM(ou...  19.5 us
    pallas_call x1, Pallas kernels, shards(): pl.pallas_call(functools.partial(write_early, sizes), out_shape=[whole] *...  5.01 us
    ppermute x1, waiting for transfers between devices, cross(): return lax.ppermute(block, 'lat', [(0, 1), (1, 0)])  3.94 us
  transfers between devices with their start and end apart: 1, of which 1 were waited for; matrix products, arithmetic and copies ran while one was open for 0% of the time, Pallas kernels for 3%

profile of v6, /device:TPU:0, one launch (start us, length us, event | category | flops | bytes accessed | tf_op | source)
XLA Modules:
  0.0 144.6 jit_solution(8119111101130653027)
XLA Ops:
  0.6 111.7 %shard_map.50 = (f32[4,128,32,128]{3,2,1,0:T(8,128)S(1)}, f32[4,32,128]{2,1,0:T(8,128)S(1)}, f32[4,32,128]{2,1,0:T(8,128)S(1)}, f32[1,128,32,128]{3,2,1,0:T(8,12...) custom-call(f32[4,128,32,128]{3,2,1,0:T(8,128)} %tracer.1, ...), custom_call_target="tpu_custom_call" | custom-call | tf_op jit(solution)/shard_map/pallas_call | solution.py:597
  112.3 2.1 %collective-permute-start = (f32[1,128,8,128]{3,2,1,0:T(8,128)S(1)}, f32[1,128,8,128]{3,2,1,0:T(8,128)S(1)}, u32[]{:S(2)}, u32[]{:S(2)}) collective-permute-start(f32[1,128,8,128]{3,2,1,0:T(8,128)S(1)} %get-tuple-element.21), channel_id=1, source_target_pairs={{0,16},{16,0},{1,17},{17,1},{2,18},{18,2},{3,19},{19,3},{4,20},{20... | collective-permute-start | bytes 1572872 | tf_op jit(solution)/shard_map/ppermute | solution.py:573
  114.4 5.0 %shard_map.52 = (f32[4,128,32,128]{3,2,1,0:T(8,128)}, f32[4,128,32,128]{3,2,1,0:T(8,128)}) custom-call(f32[4,128,32,128]{3,2,1,0:T(8,128)S(1)} %get-tuple-element.19.end, f32[4,32,128]{2,1,0:T(8,128)S(1)} %get-tuple-element.26.mean, f32[4,32,128]{2,1,0:T(8,128)S(1)} %get-tuple-element.27.scale), custom_call_target="tpu_custom_call" | custom-call | flops 4294967296 | bytes 12582912 | tf_op jit(solution)/shard_map/pallas_call | solution.py:629
  119.4 3.9 %collective-permute-done.rest_0_ = f32[1,128,8,128]{3,2,1,0:T(8,128)S(1)} collective-permute-done((f32[1,128,8,128]{3,2,1,0:T(8,128)S(1)}, f32[1,128,8,128]{3,2,1,0:T(8,128)S(1)}, u32[]{:S(2)}, u32[]{:S(2)}) %collective-permute-start) | collective-permute-done | bytes 524320 | tf_op jit(solution)/shard_map/ppermute | solution.py:573
  123.4 19.5 %shard_map.51 = (f32[1,128,16,128]{3,2,1,0:T(8,128)S(1)}, f32[1,128,24,128]{3,2,1,0:T(8,128)S(1)}, f32[1,8,128]{2,1,0:T(8,128)S(1)}, f32[1,8,128]{2,1,0:T(8,128)S(1)}) custom-call(f32[1,128,32,128]{3,2,1,0:T(8,128)S(1)} %get-tuple-element.16.base, f32[1,128,16,128]{3,2,1,0:T(8,128)S(1)} %get-tuple-element.17.factor, ...), custom_call_target="tpu_custom_call" | custom-call | tf_op jit(solution)/shard_map/pallas_call | solution.py:640
  142.9 1.7 %shard_map.53 = (f32[4,128,32,128]{3,2,1,0:T(8,128)}, f32[4,128,32,128]{3,2,1,0:T(8,128)}) custom-call(f32[1,128,24,128]{3,2,1,0:T(8,128)S(1)} %get-tuple-element.22.ready, f32[1,128,16,128]{3,2,1,0:T(8,128)S(1)} %get-tuple-element.23.tail, f32[1,8,128]{2,1,0:T(8,128)S(1)} %get-tuple-element.24.mean, ...), custom_call_target="tpu_custom_call", output_to_operand_aliasing={{0}: (4, {}), {1}: (5, {})} | custom-call | tf_op jit(solution)/shard_map/pallas_call | solution.py:659
Async XLA Ops:
  112.3 11.0 %collective-permute-start = (f32[1,128,8,128]{3,2,1,0:T(8,128)S(1)}, f32[1,128,8,128]{3,2,1,0:T(8,128)S(1)}, u32[]{:S(2)}, u32[]{:S(2)}) collective-permute-start(f32[1,128,8,128]{3,2,1,0:T(8,128)S(1)} %get-tuple-element.21), channel_id=1, source_target_pairs={{0,16},{16,0},{1,17},{17,1},{2,18},{18,2},{3,19},{19,3},{4,20},{20... | collective-permute-start | bytes 1572872 | tf_op jit(solution)/shard_map/ppermute | solution.py:573

commit v7 on v6

--- a/solution.py
+++ b/solution.py
@@ -12,6 +12,7 @@
 GUESS = 1.0
 TILE = 8
 ROWS = 8
+TURN = 32
 MESH = pl.DeviceIdType.MESH
 
 
@@ -89,7 +90,7 @@
         return pltpu.make_async_remote_copy(
             src_ref=field[step % 2].at[plane, rows_in, levels(chunk), :],
             dst_ref=y_halo.at[step % 2, slot, :, levels(chunk), :],
-            send_sem=y_send.at[step, chunk, s], recv_sem=y_recv.at[step, chunk, slot],
+            send_sem=y_send.at[step % 2, chunk, s], recv_sem=y_recv.at[step % 2, chunk, slot],
             device_id={"lat": peer}, device_id_type=MESH)
 
     def y_arrival(step, chunk, s):
@@ -97,7 +98,7 @@
         return pltpu.make_async_remote_copy(
             src_ref=field[step % 2].at[plane, rows_in, levels(chunk), :],
             dst_ref=y_halo.at[step % 2, s, :, levels(chunk), :],
-            send_sem=y_send.at[step, chunk, s], recv_sem=y_recv.at[step, chunk, s],
+            send_sem=y_send.at[step % 2, chunk, s], recv_sem=y_recv.at[step % 2, chunk, s],
             device_id={"lat": peer}, device_id_type=MESH)
 
     faces = [pl.ds(first, number)] + [pl.ds(side[0], 1) for side in sides]
@@ -107,7 +108,7 @@
         return pltpu.make_async_remote_copy(
             src_ref=buf.at[faces[part], I if way == 0 else 1],
             dst_ref=buf.at[faces[part], 0 if way == 0 else I + 1],
-            send_sem=x_send.at[step, way, part], recv_sem=x_recv.at[step, way, part],
+            send_sem=x_send.at[step % 2, way, part], recv_sem=x_recv.at[step % 2, way, part],
             device_id=target("lon", way), device_id_type=MESH)
 
     def z_copy(step, way, part):
@@ -115,7 +116,7 @@
         dst = z_lower if way == 0 else z_upper
         return pltpu.make_async_remote_copy(
             src_ref=src.at[step % 2, faces[part]], dst_ref=dst.at[step % 2, faces[part]],
-            send_sem=z_send.at[step, way, part], recv_sem=z_recv.at[step, way, part],
+            send_sem=z_send.at[step % 2, way, part], recv_sem=z_recv.at[step % 2, way, part],
             device_id=target("lev", way), device_id_type=MESH)
 
     def early_copy(shift):
@@ -291,13 +292,13 @@
 
     def late_part(step, chunk, s):
         plane = sides[s][0]
-        here = levels(chunk)
+        here, turn = levels(chunk), math.gcd(I, TURN)
 
         def body(b, totals):
-            r = pl.ds(b * ROWS, ROWS)
+            r = pl.ds(b * turn, turn)
             new = base[s, r, here, :] + cond[plane, r, here, :] * y_halo[step % 2, s, r, here, :]
             if step < STEPS - 1:
-                field[(step + 1) % 2][plane, pl.ds(1 + b * ROWS, ROWS), here, :] = new
+                field[(step + 1) % 2][plane, pl.ds(1 + b * turn, turn), here, :] = new
                 if step == STEPS - 2:
                     for out, (low, high) in zip(outs, cuts):
                         if low <= chunk * TILE < high:
@@ -307,9 +308,9 @@
             return tally(new, totals)
 
         if step < STEPS - 1:
-            lax.fori_loop(0, blocks, lambda b, _: body(b, 0), 0)
+            lax.fori_loop(0, I // turn, lambda b, _: body(b, 0), 0)
         else:
-            totals = lax.fori_loop(0, blocks, body, (zero, zero))
+            totals = lax.fori_loop(0, I // turn, body, (zero, zero))
             for q in range(2):
                 sums_late[chunk, s, q] = totals[q]
 
@@ -422,15 +423,15 @@
     def add(chunk, s, arrived, start):
         here = pl.ds(chunk * TILE, TILE)
         there, came = pl.ds((chunk - stay) * TILE, TILE), pl.ds(chunk * TILE - start, TILE)
-        zero = jnp.zeros((TILE, M), jnp.float32)
+        zero, turn = jnp.zeros((TILE, M), jnp.float32), math.gcd(I, TURN)
 
         def body(b, totals):
-            r = pl.ds(b * ROWS, ROWS)
+            r = pl.ds(b * turn, turn)
             new = base[s, r, here, :] + factor[s, r, there, :] * arrived[s, r, came, :]
             tail[s, r, there, :] = new
             return tally(new, totals)
 
-        totals = lax.fori_loop(0, I // ROWS, body, (zero, zero))
+        totals = lax.fori_loop(0, I // turn, body, (zero, zero))
         for q in range(2):
             sums[chunk, s, q] = totals[q]
 
@@ -611,12 +612,12 @@
             pltpu.SemaphoreType.REGULAR,
             dma((3,)),
             dma((chunks, late)),
-            dma((STEPS, chunks, late)),
-            dma((STEPS, chunks, late)),
-            dma((STEPS, 2, 1 + late)),
-            dma((STEPS, 2, 1 + late)),
-            dma((STEPS, 2, 1 + late)),
-            dma((STEPS, 2, 1 + late)),
+            dma((2, chunks, late)),
+            dma((2, chunks, late)),
+            dma((2, 2, 1 + late)),
+            dma((2, 2, 1 + late)),
+            dma((2, 2, 1 + late)),
+            dma((2, 2, 1 + late)),
             dma((peers,)),
             dma((peers,)),
         ],

time: 145 us -> 145 us (level)
  no operation moved by 1% of the time
where the time goes in v7:
time: 145 us
  Pallas kernels  137 us (94%)
  waiting for transfers between devices  4.33 us (3%)
  starting transfers between devices  2.07 us (1%)
    pallas_call x1, Pallas kernels, shards(): pl.pallas_call(functools.partial(kernel, sizes), out_shape=[pltpu.VMEM((J...  111 us
    pallas_call x1, Pallas kernels, shards(): pl.pallas_call(functools.partial(finish, sizes), out_shape=[pltpu.VMEM(ou...  19.5 us
    pallas_call x1, Pallas kernels, shards(): pl.pallas_call(functools.partial(write_early, sizes), out_shape=[whole] *...  5.01 us
    ppermute x1, waiting for transfers between devices, cross(): return lax.ppermute(block, 'lat', [(0, 1), (1, 0)])  4.33 us
  transfers between devices with their start and end apart: 1, of which 1 were waited for; matrix products, arithmetic and copies ran while one was open for 0% of the time, Pallas kernels for 3%

profile of v7, /device:TPU:0, one launch (start us, length us, event | category | flops | bytes accessed | tf_op | source)
XLA Modules:
  0.0 144.5 jit_solution(6929540834017174689)
XLA Ops:
  0.6 111.3 %shard_map.50 = (f32[4,128,32,128]{3,2,1,0:T(8,128)S(1)}, f32[4,32,128]{2,1,0:T(8,128)S(1)}, f32[4,32,128]{2,1,0:T(8,128)S(1)}, f32[1,128,32,128]{3,2,1,0:T(8,12...) custom-call(f32[4,128,32,128]{3,2,1,0:T(8,128)} %tracer.1, ...), custom_call_target="tpu_custom_call" | custom-call | tf_op jit(solution)/shard_map/pallas_call | solution.py:598
  111.9 2.1 %collective-permute-start = (f32[1,128,8,128]{3,2,1,0:T(8,128)S(1)}, f32[1,128,8,128]{3,2,1,0:T(8,128)S(1)}, u32[]{:S(2)}, u32[]{:S(2)}) collective-permute-start(f32[1,128,8,128]{3,2,1,0:T(8,128)S(1)} %get-tuple-element.21), channel_id=1, source_target_pairs={{0,16},{16,0},{1,17},{17,1},{2,18},{18,2},{3,19},{19,3},{4,20},{20... | collective-permute-start | bytes 1572872 | tf_op jit(solution)/shard_map/ppermute | solution.py:574
  114.0 5.0 %shard_map.52 = (f32[4,128,32,128]{3,2,1,0:T(8,128)}, f32[4,128,32,128]{3,2,1,0:T(8,128)}) custom-call(f32[4,128,32,128]{3,2,1,0:T(8,128)S(1)} %get-tuple-element.19.end, f32[4,32,128]{2,1,0:T(8,128)S(1)} %get-tuple-element.26.mean, f32[4,32,128]{2,1,0:T(8,128)S(1)} %get-tuple-element.27.scale), custom_call_target="tpu_custom_call" | custom-call | flops 4294967296 | bytes 12582912 | tf_op jit(solution)/shard_map/pallas_call | solution.py:630
  119.0 4.3 %collective-permute-done.rest_0_ = f32[1,128,8,128]{3,2,1,0:T(8,128)S(1)} collective-permute-done((f32[1,128,8,128]{3,2,1,0:T(8,128)S(1)}, f32[1,128,8,128]{3,2,1,0:T(8,128)S(1)}, u32[]{:S(2)}, u32[]{:S(2)}) %collective-permute-start) | collective-permute-done | bytes 524320 | tf_op jit(solution)/shard_map/ppermute | solution.py:574
  123.4 19.5 %shard_map.51 = (f32[1,128,16,128]{3,2,1,0:T(8,128)S(1)}, f32[1,128,24,128]{3,2,1,0:T(8,128)S(1)}, f32[1,8,128]{2,1,0:T(8,128)S(1)}, f32[1,8,128]{2,1,0:T(8,128)S(1)}) custom-call(f32[1,128,32,128]{3,2,1,0:T(8,128)S(1)} %get-tuple-element.16.base, f32[1,128,16,128]{3,2,1,0:T(8,128)S(1)} %get-tuple-element.17.factor, ...), custom_call_target="tpu_custom_call" | custom-call | tf_op jit(solution)/shard_map/pallas_call | solution.py:641
  142.8 1.7 %shard_map.53 = (f32[4,128,32,128]{3,2,1,0:T(8,128)}, f32[4,128,32,128]{3,2,1,0:T(8,128)}) custom-call(f32[1,128,24,128]{3,2,1,0:T(8,128)S(1)} %get-tuple-element.22.ready, f32[1,128,16,128]{3,2,1,0:T(8,128)S(1)} %get-tuple-element.23.tail, f32[1,8,128]{2,1,0:T(8,128)S(1)} %get-tuple-element.24.mean, ...), custom_call_target="tpu_custom_call", output_to_operand_aliasing={{0}: (4, {}), {1}: (5, {})} | custom-call | tf_op jit(solution)/shard_map/pallas_call | solution.py:660
Async XLA Ops:
  111.9 11.4 %collective-permute-start = (f32[1,128,8,128]{3,2,1,0:T(8,128)S(1)}, f32[1,128,8,128]{3,2,1,0:T(8,128)S(1)}, u32[]{:S(2)}, u32[]{:S(2)}) collective-permute-start(f32[1,128,8,128]{3,2,1,0:T(8,128)S(1)} %get-tuple-element.21), channel_id=1, source_target_pairs={{0,16},{16,0},{1,17},{17,1},{2,18},{18,2},{3,19},{19,3},{4,20},{20... | collective-permute-start | bytes 1572872 | tf_op jit(solution)/shard_map/ppermute | solution.py:574

commit v8 on v7

--- a/solution.py
+++ b/solution.py
@@ -61,7 +61,7 @@
     (
         even, odd, cond, sour, y_halo, z_lower, z_upper, z_first, z_last, sums_early, peer_early,
         peer_in, all_in,
-        load_sem, first_sem, y_send, y_recv, x_send, x_recv, z_send, z_recv, early_send, early_recv,
+        load_sem, first_sem, head_sem, head_send, head_recv, y_send, y_recv, x_send, x_recv, z_send, z_recv, early_send, early_recv,
     ) = rest[len(cuts):]
     n_lat, n_lon, n_lev = sizes
     J, I, K, M = tracer.shape
@@ -87,21 +87,39 @@
 
     def y_copy(step, chunk, s):
         plane, _, peer, _, slot = sides[s]
+        skip = I // 4 if step == 0 and chunk == 0 else 0
+        rows = pl.ds(skip, I - skip)
         return pltpu.make_async_remote_copy(
-            src_ref=field[step % 2].at[plane, rows_in, levels(chunk), :],
-            dst_ref=y_halo.at[step % 2, slot, :, levels(chunk), :],
+            src_ref=field[step % 2].at[plane, pl.ds(1 + skip, I - skip), levels(chunk), :],
+            dst_ref=y_halo.at[step % 2, slot, rows, levels(chunk), :],
             send_sem=y_send.at[step % 2, chunk, s], recv_sem=y_recv.at[step % 2, chunk, slot],
             device_id={"lat": peer}, device_id_type=MESH)
 
     def y_arrival(step, chunk, s):
         plane, _, peer, _, _ = sides[s]
+        skip = I // 4 if step == 0 and chunk == 0 else 0
+        rows = pl.ds(skip, I - skip)
         return pltpu.make_async_remote_copy(
-            src_ref=field[step % 2].at[plane, rows_in, levels(chunk), :],
-            dst_ref=y_halo.at[step % 2, s, :, levels(chunk), :],
+            src_ref=field[step % 2].at[plane, pl.ds(1 + skip, I - skip), levels(chunk), :],
+            dst_ref=y_halo.at[step % 2, s, rows, levels(chunk), :],
             send_sem=y_send.at[step % 2, chunk, s], recv_sem=y_recv.at[step % 2, chunk, s],
             device_id={"lat": peer}, device_id_type=MESH)
 
     faces = [pl.ds(first, number)] + [pl.ds(side[0], 1) for side in sides]
+
+    head = pl.ds(0, I // 4)
+
+    def head_load(s):
+        return pltpu.make_async_copy(
+            tracer.at[sides[s][0], head, levels(0), :], even.at[sides[s][0], pl.ds(1, I // 4), levels(0), :],
+            head_sem.at[s])
+
+    def head_copy(s, slot):
+        plane, _, peer, _, _ = sides[s]
+        return pltpu.make_async_remote_copy(
+            src_ref=even.at[plane, pl.ds(1, I // 4), levels(0), :], dst_ref=y_halo.at[0, slot, head, levels(0), :],
+            send_sem=head_send.at[s], recv_sem=head_recv.at[slot],
+            device_id={"lat": peer}, device_id_type=MESH)
 
     def x_copy(step, way, part):
         buf = field[step % 2]
@@ -131,11 +149,15 @@
     def arrives(axis, way, act):
         pl.when((below if way == 0 else above)[axis])(act)
 
-    first_loads = [[
-        pltpu.make_async_copy(
-            tracer.at[side[0], :, levels(chunk), :], even.at[side[0], rows_in, levels(chunk), :],
-            first_sem.at[chunk, s])
-        for s, side in enumerate(sides)] for chunk in range(chunks)]
+    def first_load(chunk, s):
+        skip = I // 4 if chunk == 0 else 0
+        return pltpu.make_async_copy(
+            tracer.at[sides[s][0], pl.ds(skip, I - skip), levels(chunk), :],
+            even.at[sides[s][0], pl.ds(1 + skip, I - skip), levels(chunk), :], first_sem.at[chunk, s])
+
+    first_loads = [[first_load(chunk, s) for s in range(len(sides))] for chunk in range(chunks)]
+    for s in range(len(sides)):
+        head_load(s).start()
     loads = [
         pltpu.make_async_copy(
             tracer.at[pl.ds(first, number)], even.at[pl.ds(first, number), rows_in], load_sem.at[0]),
@@ -166,6 +188,9 @@
     loads[0].start()
     pl.semaphore_wait(barrier, met)
 
+    for s, side in enumerate(sides):
+        head_load(s).wait()
+        when(side[3], lambda: head_copy(s, side[4]).start())
     for chunk in range(chunks):
         for s, side in enumerate(sides):
             first_loads[chunk][s].wait()
@@ -351,6 +376,9 @@
             faces_arrive(step, part)
         for chunk in range(chunks):
             base_part(step, chunk)
+        if step == 1:
+            for s, side in enumerate(sides):
+                when(side[3], lambda: head_copy(s, side[4]).wait_send())
         if step >= 1:
             for s, side in enumerate(sides):
                 for chunk in range(chunks):
@@ -376,6 +404,8 @@
                 early_copy(shift).wait_send()
         for chunk in range(stay if last else chunks):
             for s, side in enumerate(sides):
+                if step == 0 and chunk == 0:
+                    when(side[3], lambda: head_copy(s, s).wait_recv())
                 when(side[3], lambda: y_arrival(step, chunk, s).wait_recv())
                 late_part(step, chunk, s)
                 if step < STEPS - 2:
@@ -612,6 +642,9 @@
             pltpu.SemaphoreType.REGULAR,
             dma((3,)),
             dma((chunks, late)),
+            dma((late,)),
+            dma((late,)),
+            dma((late,)),
             dma((2, chunks, late)),
             dma((2, chunks, late)),
             dma((2, 2, 1 + late)),

time: 145 us -> 145 us (level)
  no operation moved by 1% of the time
where the time goes in v8:
time: 145 us; the launch traced here: 144 us
  Pallas kernels  137 us (94%)
  waiting for transfers between devices  4.15 us (3%)
  starting transfers between devices  2.49 us (2%)
    pallas_call x1, Pallas kernels, shards(): pl.pallas_call(functools.partial(kernel, sizes), out_shape=[pltpu.VMEM((J...  111 us
    pallas_call x1, Pallas kernels, shards(): pl.pallas_call(functools.partial(finish, sizes), out_shape=[pltpu.VMEM(ou...  19.3 us
    pallas_call x1, Pallas kernels, shards(): pl.pallas_call(functools.partial(write_early, sizes), out_shape=[whole] *...  5.01 us
    ppermute x1, waiting for transfers between devices, cross(): return lax.ppermute(block, 'lat', [(0, 1), (1, 0)])  4.15 us
  transfers between devices with their start and end apart: 1, of which 1 were waited for; matrix products, arithmetic and copies ran while one was open for 0% of the time, Pallas kernels for 3%

profile of v8, /device:TPU:0, one launch (start us, length us, event | category | flops | bytes accessed | tf_op | source)
XLA Modules:
  0.0 144.4 jit_solution(15966809067545079222)
XLA Ops:
  0.6 111.1 %shard_map.50 = (f32[4,128,32,128]{3,2,1,0:T(8,128)S(1)}, f32[4,32,128]{2,1,0:T(8,128)S(1)}, f32[4,32,128]{2,1,0:T(8,128)S(1)}, f32[1,128,32,128]{3,2,1,0:T(8,12...) custom-call(f32[4,128,32,128]{3,2,1,0:T(8,128)} %tracer.1, ...), custom_call_target="tpu_custom_call" | custom-call | tf_op jit(solution)/shard_map/pallas_call | solution.py:628
  111.7 2.5 %collective-permute-start = (f32[1,128,8,128]{3,2,1,0:T(8,128)S(1)}, f32[1,128,8,128]{3,2,1,0:T(8,128)S(1)}, u32[]{:S(2)}, u32[]{:S(2)}) collective-permute-start(f32[1,128,8,128]{3,2,1,0:T(8,128)S(1)} %get-tuple-element.21), channel_id=1, source_target_pairs={{0,16},{16,0},{1,17},{17,1},{2,18},{18,2},{3,19},{19,3},{4,20},{20... | collective-permute-start | bytes 1572872 | tf_op jit(solution)/shard_map/ppermute | solution.py:604
  114.2 5.0 %shard_map.52 = (f32[4,128,32,128]{3,2,1,0:T(8,128)}, f32[4,128,32,128]{3,2,1,0:T(8,128)}) custom-call(f32[4,128,32,128]{3,2,1,0:T(8,128)S(1)} %get-tuple-element.19.end, f32[4,32,128]{2,1,0:T(8,128)S(1)} %get-tuple-element.26.mean, f32[4,32,128]{2,1,0:T(8,128)S(1)} %get-tuple-element.27.scale), custom_call_target="tpu_custom_call" | custom-call | flops 4294967296 | bytes 12582912 | tf_op jit(solution)/shard_map/pallas_call | solution.py:663
  119.2 4.2 %collective-permute-done.rest_0_ = f32[1,128,8,128]{3,2,1,0:T(8,128)S(1)} collective-permute-done((f32[1,128,8,128]{3,2,1,0:T(8,128)S(1)}, f32[1,128,8,128]{3,2,1,0:T(8,128)S(1)}, u32[]{:S(2)}, u32[]{:S(2)}) %collective-permute-start) | collective-permute-done | bytes 524320 | tf_op jit(solution)/shard_map/ppermute | solution.py:604
  123.4 19.3 %shard_map.51 = (f32[1,128,16,128]{3,2,1,0:T(8,128)S(1)}, f32[1,128,24,128]{3,2,1,0:T(8,128)S(1)}, f32[1,8,128]{2,1,0:T(8,128)S(1)}, f32[1,8,128]{2,1,0:T(8,128)S(1)}) custom-call(f32[1,128,32,128]{3,2,1,0:T(8,128)S(1)} %get-tuple-element.16.base, f32[1,128,16,128]{3,2,1,0:T(8,128)S(1)} %get-tuple-element.17.factor, ...), custom_call_target="tpu_custom_call" | custom-call | tf_op jit(solution)/shard_map/pallas_call | solution.py:674
  142.7 1.7 %shard_map.53 = (f32[4,128,32,128]{3,2,1,0:T(8,128)}, f32[4,128,32,128]{3,2,1,0:T(8,128)}) custom-call(f32[1,128,24,128]{3,2,1,0:T(8,128)S(1)} %get-tuple-element.22.ready, f32[1,128,16,128]{3,2,1,0:T(8,128)S(1)} %get-tuple-element.23.tail, f32[1,8,128]{2,1,0:T(8,128)S(1)} %get-tuple-element.24.mean, ...), custom_call_target="tpu_custom_call", output_to_operand_aliasing={{0}: (4, {}), {1}: (5, {})} | custom-call | tf_op jit(solution)/shard_map/pallas_call | solution.py:693
Async XLA Ops:
  111.7 11.7 %collective-permute-start = (f32[1,128,8,128]{3,2,1,0:T(8,128)S(1)}, f32[1,128,8,128]{3,2,1,0:T(8,128)S(1)}, u32[]{:S(2)}, u32[]{:S(2)}) collective-permute-start(f32[1,128,8,128]{3,2,1,0:T(8,128)S(1)} %get-tuple-element.21), channel_id=1, source_target_pairs={{0,16},{16,0},{1,17},{17,1},{2,18},{18,2},{3,19},{19,3},{4,20},{20... | collective-permute-start | bytes 1572872 | tf_op jit(solution)/shard_map/ppermute | solution.py:604

commit v9 on v8

--- a/solution.py
+++ b/solution.py
@@ -466,13 +466,13 @@
             sums[chunk, s, q] = totals[q]
 
     barrier = pltpu.get_barrier_semaphore()
-    met = jnp.where(even_lon, n_lon - n_odd - 1, n_lon - 1)
+    met = jnp.where(even_lon, 0, n_lon - 1)
     for _, _, peer, exists, _ in sides:
         when(exists, lambda: pl.semaphore_signal(
             barrier, inc=1, device_id={"lat": peer}, device_id_type=MESH))
         met = met + (1 if exists is None else exists.astype(jnp.int32))
     for peer in peers:
-        pl.when(jnp.logical_or(even_lon, peer % 2 == 1))(lambda: pl.semaphore_signal(
+        pl.when(peer % 2 == 1)(lambda: pl.semaphore_signal(
             barrier, inc=1, device_id={"lon": peer}, device_id_type=MESH))
     pl.semaphore_wait(barrier, met)
     for s, side in enumerate(sides):

time: 145 us -> 145 us (level)
  no operation moved by 1% of the time
where the time goes in v9:
time: 145 us; the launch traced here: 144 us
  Pallas kernels  137 us (94%)
  waiting for transfers between devices  4.15 us (3%)
  starting transfers between devices  2.49 us (2%)
    pallas_call x1, Pallas kernels, shards(): pl.pallas_call(functools.partial(kernel, sizes), out_shape=[pltpu.VMEM((J...  111 us
    pallas_call x1, Pallas kernels, shards(): pl.pallas_call(functools.partial(finish, sizes), out_shape=[pltpu.VMEM(ou...  19.3 us
    pallas_call x1, Pallas kernels, shards(): pl.pallas_call(functools.partial(write_early, sizes), out_shape=[whole] *...  5.01 us
    ppermute x1, waiting for transfers between devices, cross(): return lax.ppermute(block, 'lat', [(0, 1), (1, 0)])  4.15 us
  transfers between devices with their start and end apart: 1, of which 1 were waited for; matrix products, arithmetic and copies ran while one was open for 0% of the time, Pallas kernels for 3%

profile of v9, /device:TPU:0, one launch (start us, length us, event | category | flops | bytes accessed | tf_op | source)
XLA Modules:
  0.0 144.4 jit_solution(16135089919153588945)
XLA Ops:
  0.6 111.1 %shard_map.50 = (f32[4,128,32,128]{3,2,1,0:T(8,128)S(1)}, f32[4,32,128]{2,1,0:T(8,128)S(1)}, f32[4,32,128]{2,1,0:T(8,128)S(1)}, f32[1,128,32,128]{3,2,1,0:T(8,12...) custom-call(f32[4,128,32,128]{3,2,1,0:T(8,128)} %tracer.1, ...), custom_call_target="tpu_custom_call" | custom-call | tf_op jit(solution)/shard_map/pallas_call | solution.py:628
  111.7 2.5 %collective-permute-start = (f32[1,128,8,128]{3,2,1,0:T(8,128)S(1)}, f32[1,128,8,128]{3,2,1,0:T(8,128)S(1)}, u32[]{:S(2)}, u32[]{:S(2)}) collective-permute-start(f32[1,128,8,128]{3,2,1,0:T(8,128)S(1)} %get-tuple-element.21), channel_id=1, source_target_pairs={{0,16},{16,0},{1,17},{17,1},{2,18},{18,2},{3,19},{19,3},{4,20},{20... | collective-permute-start | bytes 1572872 | tf_op jit(solution)/shard_map/ppermute | solution.py:604
  114.2 5.0 %shard_map.52 = (f32[4,128,32,128]{3,2,1,0:T(8,128)}, f32[4,128,32,128]{3,2,1,0:T(8,128)}) custom-call(f32[4,128,32,128]{3,2,1,0:T(8,128)S(1)} %get-tuple-element.19.end, f32[4,32,128]{2,1,0:T(8,128)S(1)} %get-tuple-element.26.mean, f32[4,32,128]{2,1,0:T(8,128)S(1)} %get-tuple-element.27.scale), custom_call_target="tpu_custom_call" | custom-call | flops 4294967296 | bytes 12582912 | tf_op jit(solution)/shard_map/pallas_call | solution.py:663
  119.2 4.2 %collective-permute-done.rest_0_ = f32[1,128,8,128]{3,2,1,0:T(8,128)S(1)} collective-permute-done((f32[1,128,8,128]{3,2,1,0:T(8,128)S(1)}, f32[1,128,8,128]{3,2,1,0:T(8,128)S(1)}, u32[]{:S(2)}, u32[]{:S(2)}) %collective-permute-start) | collective-permute-done | bytes 524320 | tf_op jit(solution)/shard_map/ppermute | solution.py:604
  123.4 19.3 %shard_map.51 = (f32[1,128,16,128]{3,2,1,0:T(8,128)S(1)}, f32[1,128,24,128]{3,2,1,0:T(8,128)S(1)}, f32[1,8,128]{2,1,0:T(8,128)S(1)}, f32[1,8,128]{2,1,0:T(8,128)S(1)}) custom-call(f32[1,128,32,128]{3,2,1,0:T(8,128)S(1)} %get-tuple-element.16.base, f32[1,128,16,128]{3,2,1,0:T(8,128)S(1)} %get-tuple-element.17.factor, ...), custom_call_target="tpu_custom_call" | custom-call | tf_op jit(solution)/shard_map/pallas_call | solution.py:674
  142.7 1.7 %shard_map.53 = (f32[4,128,32,128]{3,2,1,0:T(8,128)}, f32[4,128,32,128]{3,2,1,0:T(8,128)}) custom-call(f32[1,128,24,128]{3,2,1,0:T(8,128)S(1)} %get-tuple-element.22.ready, f32[1,128,16,128]{3,2,1,0:T(8,128)S(1)} %get-tuple-element.23.tail, f32[1,8,128]{2,1,0:T(8,128)S(1)} %get-tuple-element.24.mean, ...), custom_call_target="tpu_custom_call", output_to_operand_aliasing={{0}: (4, {}), {1}: (5, {})} | custom-call | tf_op jit(solution)/shard_map/pallas_call | solution.py:693
Async XLA Ops:
  111.7 11.7 %collective-permute-start = (f32[1,128,8,128]{3,2,1,0:T(8,128)S(1)}, f32[1,128,8,128]{3,2,1,0:T(8,128)S(1)}, u32[]{:S(2)}, u32[]{:S(2)}) collective-permute-start(f32[1,128,8,128]{3,2,1,0:T(8,128)S(1)} %get-tuple-element.21), channel_id=1, source_target_pairs={{0,16},{16,0},{1,17},{17,1},{2,18},{18,2},{3,19},{19,3},{4,20},{20... | collective-permute-start | bytes 1572872 | tf_op jit(solution)/shard_map/ppermute | solution.py:604
